TPU v7x, 256 devices: a whole 4x4x8 slice. The times are simulated.
256 devices in a mesh: wall: 8 (over z), span: 32 (over x, y, core).
Axes of the slice: x: 4, y: 4, z: 8, core: 2. Of those that a mesh axis runs over, the one named last changes fastest.
Arguments:
- noise_bits: int32 [3, 32, 2048, 2048], P(None, None, 'span', 'wall'), may hold values from 0 to 1073741823
- filter_widths: int32 [2048], P('wall'), may hold values from 8 to 64, as said below
- target_mean_profile: float32 [3, 2048], P(None, 'wall'), may hold values from -4 to 4
- target_factor_diagonal: float32 [3, 2048], P(None, 'wall'), may hold values from 0.3 to 2
- target_factor_lower: float32 [3, 2048], P(None, 'wall'), may hold values from -0.8 to 0.8
Outputs:
- inflow_field: float32 [3, 32, 2048, 2048], P(None, None, 'span', 'wall')
Inputs may be any that keep to these rules, and one draw needn't show every extreme that they name: `filter_widths`: every row's width lies between 8 and 64, and both ends occur in every draw.
All inputs are finite; a program needn't handle non-finite values.
Results may differ from a plain program's by a relative error of at most 0.0045.
Values may be sent and summed in bfloat16 or wider, within the bound.
A program may use at most 64 MiB of HBM per device.

v0:
```python
import math

import jax
import jax.numpy as jnp
from jax import lax
from jax.sharding import PartitionSpec as P

WMAX = 64
SPANW = 32
TSCALE = 8


PAIRS = ((0, 0), (1, 0), (1, 1), (2, 0), (2, 1), (2, 2))
SPREAD_FLOOR = 0.25
INV_RANGE = 1.0 / 1073741824.0


def padded_2(cells, sides, width, closed):
    for axis, dim in sides:
        count = lax.axis_size(axis)
        ends = count if closed else count - 1
        head = lax.slice_in_dim(cells, 0, width, axis=dim)
        tail = lax.slice_in_dim(cells, cells.shape[dim] - width, cells.shape[dim], axis=dim)
        cells = jnp.concatenate(
            [
                lax.ppermute(tail, axis, [(i, (i + 1) % count) for i in range(ends)]),
                cells,
                lax.ppermute(head, axis, [((i + 1) % count, i) for i in range(ends)]),
            ],
            axis=dim,
        )
    return cells


def copy_for_each(array, axis):
    count = lax.axis_size(axis)
    return lax.all_to_all(
        jnp.broadcast_to(array[None], (count, *array.shape)), axis, 0, 0, tiled=True
    )


def of_everyone(array, axis):
    everything = copy_for_each(array, axis)
    return jnp.sum(everything, axis=0)


def packed_total(arrays, axis):
    ravelled, at, gathered = (jnp.concatenate([a.reshape(-1) for a in arrays]), 0, [])
    running = of_everyone(ravelled, axis)
    for a in arrays:
        gathered.append(running[at : at + a.size].reshape(a.shape))
        at += a.size
    return tuple(gathered)


def to_field(noise_bits):
    scaled = (noise_bits.astype(jnp.float32) + 0.5) * INV_RANGE - 0.5
    return (math.sqrt(12.0) * scaled).astype(jnp.bfloat16)


def band_matrix(cell_widths, in_count, margin):
    out_count = cell_widths.shape[0]
    offsets = (
        lax.broadcasted_iota(jnp.int32, (out_count, in_count), 1)
        - margin
        - lax.broadcasted_iota(jnp.int32, (out_count, in_count), 0)
    ).astype(jnp.float32)
    spread = cell_widths[:, None]
    inside = jnp.abs(offsets) <= 2.0 * spread
    safe_off = jnp.where(inside, offsets, 0.0)
    kernel = jnp.where(
        inside, jnp.exp(-math.pi * safe_off * safe_off / (8.0 * spread * spread)), 0.0
    )
    norm_total = jnp.sqrt(jnp.sum(kernel * kernel, axis=1, keepdims=True))
    return (kernel / norm_total).astype(jnp.bfloat16)


def time_matrix(sample_count):
    later_idx = lax.broadcasted_iota(jnp.int32, (sample_count, sample_count), 0)
    earlier = lax.broadcasted_iota(jnp.int32, (sample_count, sample_count), 1)
    causal = later_idx >= earlier
    lagged = jnp.where(causal, later_idx - earlier, 0).astype(jnp.float32)
    decay_rate = math.exp(-math.pi / (2.0 * TSCALE))
    fresh_gain = jnp.where(earlier == 0, 1.0, math.sqrt(1.0 - decay_rate * decay_rate))
    return jnp.where(causal, jnp.exp(-math.pi * lagged / (2.0 * TSCALE)) * fresh_gain, 0.0)


def lund_transform(sample_covariance, target_factor_diagonal, target_factor_lower):
    cov_00 = sample_covariance[0] + SPREAD_FLOOR
    cov_10 = sample_covariance[1]
    cov_11 = sample_covariance[2] + SPREAD_FLOOR
    cov_20 = sample_covariance[3]
    cov_21 = sample_covariance[4]
    cov_22 = sample_covariance[5] + SPREAD_FLOOR
    chol_00 = jnp.sqrt(cov_00)
    chol_10 = cov_10 / chol_00
    chol_20 = cov_20 / chol_00
    chol_11 = jnp.sqrt(cov_11 - chol_10 * chol_10)
    chol_21 = (cov_21 - chol_20 * chol_10) / chol_11
    chol_22 = jnp.sqrt(cov_22 - chol_20 * chol_20 - chol_21 * chol_21)
    inv_00 = 1.0 / chol_00
    inv_11 = 1.0 / chol_11
    inv_22 = 1.0 / chol_22
    inv_10 = -chol_10 * inv_00 * inv_11
    inv_21 = -chol_21 * inv_11 * inv_22
    inv_20 = -(chol_20 * inv_00 + chol_21 * inv_10) * inv_22
    gain_00 = target_factor_diagonal[0] * inv_00
    gain_10 = target_factor_lower[0] * inv_00 + target_factor_diagonal[1] * inv_10
    gain_11 = target_factor_diagonal[1] * inv_11
    gain_20 = (
        target_factor_lower[1] * inv_00
        + target_factor_lower[2] * inv_10
        + target_factor_diagonal[2] * inv_20
    )
    gain_21 = target_factor_lower[2] * inv_11 + target_factor_diagonal[2] * inv_21
    gain_22 = target_factor_diagonal[2] * inv_22
    return jnp.stack([gain_00, gain_10, gain_11, gain_20, gain_21, gain_22])


def rescaled_inflow(fluctuation, per_row_means, scaling_terms, velocity_profile):
    centred_samples = fluctuation - per_row_means[:, None, None, :]
    first_component = velocity_profile[0] + scaling_terms[0] * centred_samples[0]
    second_component = (
        velocity_profile[1]
        + scaling_terms[1] * centred_samples[0]
        + scaling_terms[2] * centred_samples[1]
    )
    third_component = (
        velocity_profile[2]
        + scaling_terms[3] * centred_samples[0]
        + scaling_terms[4] * centred_samples[1]
        + scaling_terms[5] * centred_samples[2]
    )
    return jnp.stack([first_component, second_component, third_component])


def pair_sums(values):
    return jnp.stack(
        [jnp.sum(values[first_c] * values[second_c], axis=(0, 1)) for first_c, second_c in PAIRS]
    )


def raw_spread(moments, per_row_means):
    return jnp.stack(
        [
            moments[slot] - per_row_means[first_c] * per_row_means[second_c]
            for slot, (first_c, second_c) in enumerate(PAIRS)
        ]
    )


def span_filter(widened, span_band):
    return jnp.einsum("kj,csjy->csky", span_band, widened, preferred_element_type=jnp.float32)


def time_filter(spanned, memory):
    return jnp.einsum("ts,csky->ctky", memory, spanned)


def shards(
    noise_bits, filter_widths, target_mean_profile, target_factor_diagonal, target_factor_lower
):
    n_comp, n_samples, n_cols, n_rows = noise_bits.shape
    span_count = lax.axis_size("span")
    margin = 2 * WMAX
    span_margin = 2 * SPANW
    psi_field = to_field(noise_bits)
    padded = padded_2(psi_field, (("wall", 3),), margin, False)
    wall_band = band_matrix(filter_widths.astype(jnp.float32), n_rows + 2 * margin, margin)
    smooth = jnp.einsum(
        "csjm,ym->csjy", padded, wall_band, preferred_element_type=jnp.float32
    ).astype(jnp.bfloat16)
    span_band = band_matrix(
        jnp.full((n_cols,), float(SPANW), jnp.float32), n_cols + 2 * span_margin, span_margin
    )
    memory = time_matrix(n_samples)
    cell_count = float(n_samples * n_cols * span_count)
    widened = padded_2(smooth, (("span", 2),), span_margin, True)
    fluctuation = time_filter(span_filter(widened, span_band), memory)
    local_sums = jnp.sum(fluctuation, axis=(1, 2))
    total_sums, total_pairs = packed_total((local_sums, pair_sums(fluctuation)), "span")
    per_row_means = total_sums / cell_count
    sample_covariance = raw_spread(total_pairs / cell_count, per_row_means)
    scaling_terms = lund_transform(sample_covariance, target_factor_diagonal, target_factor_lower)
    return rescaled_inflow(fluctuation, per_row_means, scaling_terms, target_mean_profile)


def solution(mesh):
    placed = (
        P(None, None, "span", "wall"),
        P("wall"),
        P(None, "wall"),
        P(None, "wall"),
        P(None, "wall"),
    )
    return jax.shard_map(
        shards, mesh=mesh, in_specs=placed, out_specs=P(None, None, "span", "wall"), check_vma=False
    )
```

profile of v0, /device:TPU:97, one launch (start us, length us, event | category | flops | bytes accessed | tf_op | source)
XLA Modules:
  0.0 129.0 jit_solution(15216082362230762508)
XLA Ops:
  0.0 3.9 %multiply_convert_fusion = bf16[3,32,64,256]{3,2,1,0:T(8,128)(2,1)S(1)} fusion(s32[3,32,64,256]{3,2,1,0:T(8,128)} %param.5), kind=kLoop, calls=%fused_computation.15 | loop fusion | flops 9437184 | bytes 9437184 | tf_op jit(solution)/shard_map/convert_element_type | solution.py:58
  3.9 0.0 copy-start.4
  4.0 0.9 fusion.72
  4.9 4.8 %collective-permute-start = (bf16[3,32,64,128]{3,2,1,0:T(8,128)(2,1)S(1)}, bf16[3,32,64,128]{3,2,1,0:T(8,128)(2,1)S(1)}, u32[]{:S(2)}, u32[]{:S(2)}) collective-permute-start(bf16[3,32,64,128]{3,2,1,0:T(8,128)(2,1)S(1)} %get-tuple-element.22), channel_id=1, source_target_pairs={{0,32},{32,64},{64,96},{96,128},{128,160},{160,192},{192,224},{1,3... | collective-permute-start | bytes 4718600 | tf_op jit(solution)/shard_map/ppermute | solution.py:26
  9.7 1.9 %collective-permute-start.1 = (bf16[3,32,64,128]{3,2,1,0:T(8,128)(2,1)S(1)}, bf16[3,32,64,128]{3,2,1,0:T(8,128)(2,1)S(1)}, u32[]{:S(2)}, u32[]{:S(2)}) collective-permute-start(bf16[3,32,64,128]{3,2,1,0:T(8,128)(2,1)S(1)} %get-tuple-element.23), channel_id=1, source_target_pairs={{32,0},{64,32},{96,64},{128,96},{160,128},{192,160},{224,192},{33,... | collective-permute-start | bytes 4718600 | tf_op jit(solution)/shard_map/ppermute | solution.py:28
  11.6 0.0 copy-done.4
  11.6 0.4 multiply_reduce_fusion.6
  12.0 0.0 copy-start.1
  12.0 30.7 %collective-permute-done = bf16[3,32,64,128]{3,2,1,0:T(8,128)(2,1)S(1)} collective-permute-done((bf16[3,32,64,128]{3,2,1,0:T(8,128)(2,1)S(1)}, bf16[3,32,64,128]{3,2,1,0:T(8,128)(2,1)S(1)}, u32[]{:S(2)}, u32[]{:S(2)}) %collective-permute-start) | collective-permute-done | bytes 1572896 | tf_op jit(solution)/shard_map/ppermute | solution.py:26
  42.7 5.0 %collective-permute-done.1 = bf16[3,32,64,128]{3,2,1,0:T(8,128)(2,1)S(1)} collective-permute-done((bf16[3,32,64,128]{3,2,1,0:T(8,128)(2,1)S(1)}, bf16[3,32,64,128]{3,2,1,0:T(8,128)(2,1)S(1)}, u32[]{:S(2)}, u32[]{:S(2)}) %collective-permute-start.1) | collective-permute-done | bytes 1572896 | tf_op jit(solution)/shard_map/ppermute | solution.py:28
  47.8 2.5 %fusion.20 = bf16[3,32,64,256]{3,2,1,0:T(8,128)(2,1)S(1)} fusion(bf16[3,32,64,128]{3,2,1,0:T(8,128)(2,1)S(1)} %collective-permute-done.1, bf16[3,32,64,256]{3,2,1,0:T(8,128)(2,1)S(1)} %multiply_convert_fusion, bf16[3,32,64,128]{3,2,1,0:T(8,128)(2,1)S(1)} %collective-permute-done, f32[256]{0:T(256)S(1)} %sqrt.58, f32[256]{0:T(256)S(1)} %get-tuple-element.38, ...), kind=kOutput, calls=%fused_computation.19 | convolution fusion | flops 1632501760 | bytes 9442304 | tf_op jit(solution)/shard_map/csjm,ym->csjy/dot_general | solution.py:170
  50.3 3.1 %collective-permute-start.2 = (bf16[3,32,64,256]{3,2,1,0:T(8,128)(2,1)S(1)}, bf16[3,32,64,256]{3,2,1,0:T(8,128)(2,1)S(1)}, u32[]{:S(2)}, u32[]{:S(2)}) collective-permute-start(bf16[3,32,64,256]{3,2,1,0:T(8,128)(2,1)S(1)} %fusion.20), channel_id=1, source_target_pairs={{0,1},{1,2},{2,3},{3,4},{4,5},{5,6},{6,7},{7,8},{8,9},{9,10},{10,1... | collective-permute-start | bytes 9437192 | tf_op jit(solution)/shard_map/ppermute | solution.py:26
  53.3 0.0 collective-permute-start.3
  53.3 0.1 multiply_reduce_fusion.7
  53.5 0.0 copy-done.1
  53.5 34.0 %collective-permute-done.2 = bf16[3,32,64,256]{3,2,1,0:T(8,128)(2,1)S(1)} collective-permute-done((bf16[3,32,64,256]{3,2,1,0:T(8,128)(2,1)S(1)}, bf16[3,32,64,256]{3,2,1,0:T(8,128)(2,1)S(1)}, u32[]{:S(2)}, u32[]{:S(2)}) %collective-permute-start.2) | collective-permute-done | bytes 3145760 | tf_op jit(solution)/shard_map/ppermute | solution.py:26
  87.6 2.8 %collective-permute-done.3 = bf16[3,32,64,256]{3,2,1,0:T(8,128)(2,1)S(1)} collective-permute-done((bf16[3,32,64,256]{3,2,1,0:T(8,128)(2,1)S(1)}, bf16[3,32,64,256]{3,2,1,0:T(8,128)(2,1)S(1)}, u32[]{:S(2)}, u32[]{:S(2)}) %collective-permute-start.3) | collective-permute-done | bytes 3145760 | tf_op jit(solution)/shard_map/ppermute | solution.py:28
  90.3 2.5 %fusion.17 = bf16[3,32,64,256]{3,2,1,0:T(8,128)(2,1)S(1)} fusion(bf16[3,32,64,256]{3,2,1,0:T(8,128)(2,1)S(1)} %collective-permute-done.3, bf16[3,32,64,256]{3,2,1,0:T(8,128)(2,1)S(1)} %fusion.20, bf16[3,32,64,256]{3,2,1,0:T(8,128)(2,1)S(1)} %collective-permute-done.2, f32[64]{0:T(128)S(1)} %sqrt.59, s32[192]{0:T(256)S(1)} %iota_add_fusion.1), kind=kOutput, calls=%fused_computation.18 | convolution fusion | flops 632426496 | bytes 12583936 | tf_op jit(solution)/shard_map/kj,csjy->csky/dot_general | solution.py:153
  92.8 2.1 %fusion.76 = (f32[3,256]{1,0:T(4,128)S(1)}, f32[3,32,64,256]{3,1,2,0:T(8,128)S(1)}) fusion(f32[32]{0:T(128)S(1)} %compare_select_fusion, bf16[3,32,64,256]{3,2,1,0:T(8,128)(2,1)S(1)} %fusion.17), kind=kOutput, calls=%fused_computation.113 | convolution fusion | flops 102242560 | bytes 9440384 | tf_op jit(solution)/shard_map/ts,csky->ctky/dot_general | solution.py:157
  94.9 0.0 copy-start
  94.9 0.0 copy-start.2
  94.9 0.0 copy-start.3
  94.9 0.9 multiply_reduce_fusion
  95.8 1.8 %copy-done = f32[3,32,64,256]{3,1,2,0:T(8,128)} copy-done((f32[3,32,64,256]{3,1,2,0:T(8,128)}, f32[3,32,64,256]{3,1,2,0:T(8,128)S(1)}, u32[]{:S(2)}) %copy-start) | copy-done | bytes 6291480
  97.7 0.9 broadcast_in_dim.45
  98.5 8.4 %all-to-all-start = ((f32[32,1,2304]{2,1,0:T(1,128)}), f32[32,1,2304]{2,1,0:T(1,128)S(1)}, u32[]{:S(2)}, u32[]{:S(2)}) async-start(f32[32,1,2304]{2,1,0:T(1,128)} %broadcast_in_dim.45), calls=%async_computation | async-start | bytes 589824 | tf_op jit(solution)/shard_map/all_to_all | solution.py:37
  106.9 0.0 copy-done.2
  106.9 0.0 copy-done.3
  106.9 9.2 %all-to-all-done = f32[32,1,2304]{2,1,0:T(1,128)S(1)} async-done(((f32[32,1,2304]{2,1,0:T(1,128)}), f32[32,1,2304]{2,1,0:T(1,128)S(1)}, u32[]{:S(2)}, u32[]{:S(2)}) %all-to-all-start) | async-done | bytes 294944 | tf_op jit(solution)/shard_map/all_to_all | solution.py:37
  116.2 0.2 reduce_sum.99
  116.4 3.5 %broadcast_subtract_fusion = f32[3,32,64,256]{3,1,2,0:T(8,128)S(1)} fusion(f32[3,32,64,256]{3,1,2,0:T(8,128)} %copy-done, f32[3,256]{1,0:T(4,128)S(1)} %div.135), kind=kLoop, calls=%fused_computation.16 | loop fusion | flops 1572864 | bytes 12585984 | tf_op jit(solution)/shard_map/sub | solution.py:121
  120.0 1.5 %multiply_add_fusion.1 = (f32[1,32,64,256]{3,1,2,0:T(8,128)S(1)}, f32[1,32,64,256]{3,1,2,0:T(8,128)S(1)}, f32[1,32,64,256]{3,1,2,0:T(8,128)S(1)}) fusion(f32[3,32,64,256]{3,1,2,0:T(8,128)S(1)} %broadcast_subtract_fusion, f32[256]{0:T(256)S(1)} %get-tuple-element.11, f32[256]{0:T(256)S(1)} %bitcast.46, f32[256]{0:T(256)S(1)} %get-tuple-element.30, ...), kind=kLoop, calls=%fused_computation.23 | loop fusion | flops 6291456 | bytes 12592128 | tf_op jit(solution)/shard_map/add | solution.py:122
  121.6 1.1 pad_maximum_fusion
  122.7 6.4 %copy.10 = f32[3,32,64,256]{3,2,1,0:T(8,128)} copy(f32[3,32,64,256]{3,1,2,0:T(8,128)S(1)} %pad_maximum_fusion) | data formatting | bytes 12582912 | tf_op jit(solution)/shard_map/stack | solution.py:134
  (20 shorter events, 0.2 us)
Async XLA Ops:
  3.9 7.7 %copy-start.4 = (s32[256]{0:T(256)S(1)}, s32[256]{0:T(256)}, u32[]{:S(2)}) copy-start(s32[256]{0:T(256)} %param.6) | copy-start | bytes 3076
  4.9 37.8 %collective-permute-start = (bf16[3,32,64,128]{3,2,1,0:T(8,128)(2,1)S(1)}, bf16[3,32,64,128]{3,2,1,0:T(8,128)(2,1)S(1)}, u32[]{:S(2)}, u32[]{:S(2)}) collective-permute-start(bf16[3,32,64,128]{3,2,1,0:T(8,128)(2,1)S(1)} %get-tuple-element.22), channel_id=1, source_target_pairs={{0,32},{32,64},{64,96},{96,128},{128,160},{160,192},{192,224},{1,3... | collective-permute-start | bytes 4718600 | tf_op jit(solution)/shard_map/ppermute | solution.py:26
  9.7 38.1 %collective-permute-start.1 = (bf16[3,32,64,128]{3,2,1,0:T(8,128)(2,1)S(1)}, bf16[3,32,64,128]{3,2,1,0:T(8,128)(2,1)S(1)}, u32[]{:S(2)}, u32[]{:S(2)}) collective-permute-start(bf16[3,32,64,128]{3,2,1,0:T(8,128)(2,1)S(1)} %get-tuple-element.23), channel_id=1, source_target_pairs={{32,0},{64,32},{96,64},{128,96},{160,128},{192,160},{224,192},{33,... | collective-permute-start | bytes 4718600 | tf_op jit(solution)/shard_map/ppermute | solution.py:28
  12.0 41.5 %copy-start.1 = (f32[3,256]{1,0:T(4,128)S(1)}, f32[3,256]{1,0:T(4,128)}, u32[]{:S(2)}) copy-start(f32[3,256]{1,0:T(4,128)} %param.8) | copy-start | bytes 9220
  50.3 37.3 %collective-permute-start.2 = (bf16[3,32,64,256]{3,2,1,0:T(8,128)(2,1)S(1)}, bf16[3,32,64,256]{3,2,1,0:T(8,128)(2,1)S(1)}, u32[]{:S(2)}, u32[]{:S(2)}) collective-permute-start(bf16[3,32,64,256]{3,2,1,0:T(8,128)(2,1)S(1)} %fusion.20), channel_id=1, source_target_pairs={{0,1},{1,2},{2,3},{3,4},{4,5},{5,6},{6,7},{7,8},{8,9},{9,10},{10,1... | collective-permute-start | bytes 9437192 | tf_op jit(solution)/shard_map/ppermute | solution.py:26
  53.3 37.0 %collective-permute-start.3 = (bf16[3,32,64,256]{3,2,1,0:T(8,128)(2,1)S(1)}, bf16[3,32,64,256]{3,2,1,0:T(8,128)(2,1)S(1)}, u32[]{:S(2)}, u32[]{:S(2)}) collective-permute-start(bf16[3,32,64,256]{3,2,1,0:T(8,128)(2,1)S(1)} %fusion.20), channel_id=1, source_target_pairs={{1,0},{2,1},{3,2},{4,3},{5,4},{6,5},{7,6},{8,7},{9,8},{10,9},{11,1... | collective-permute-start | bytes 9437192 | tf_op jit(solution)/shard_map/ppermute | solution.py:28
  94.9 2.7 %copy-start = (f32[3,32,64,256]{3,1,2,0:T(8,128)}, f32[3,32,64,256]{3,1,2,0:T(8,128)S(1)}, u32[]{:S(2)}) copy-start(f32[3,32,64,256]{3,1,2,0:T(8,128)S(1)} %get-tuple-element.40) | copy-start | bytes 18874372
  94.9 12.0 %copy-start.2 = (f32[3,256]{1,0:T(4,128)S(1)}, f32[3,256]{1,0:T(4,128)}, u32[]{:S(2)}) copy-start(f32[3,256]{1,0:T(4,128)} %param.9) | copy-start | bytes 9220
  94.9 12.0 %copy-start.3 = (f32[3,256]{1,0:T(4,128)S(1)}, f32[3,256]{1,0:T(4,128)}, u32[]{:S(2)}) copy-start(f32[3,256]{1,0:T(4,128)} %param.7) | copy-start | bytes 9220
  98.5 17.6 %all-to-all-start = ((f32[32,1,2304]{2,1,0:T(1,128)}), f32[32,1,2304]{2,1,0:T(1,128)S(1)}, u32[]{:S(2)}, u32[]{:S(2)}) async-start(f32[32,1,2304]{2,1,0:T(1,128)} %broadcast_in_dim.45), calls=%async_computation | async-start | bytes 589824 | tf_op jit(solution)/shard_map/all_to_all | solution.py:37
where the time goes:
time: 129 us
  waiting for transfers between devices  81.8 us (63%)
  starting transfers between devices  18.1 us (14%)
  other arithmetic  11.8 us (9%)
  local copies, waits for them, and re-layouts  10.1 us (8%)
  matrix products  7.06 us (5%)
    ppermute x2, waiting for transfers between devices, padded_2(): lax.ppermute(tail, axis, [(i, (i + 1) % count) for i in range(ends)])  64.7 us
    all_to_all x1, waiting for transfers between devices, copy_for_each(): lax.all_to_all(jnp.broadcast_to(array[None], (count, *array.shape)), axis...  9.24 us
    all_to_all x1, starting transfers between devices, copy_for_each(): lax.all_to_all(jnp.broadcast_to(array[None], (count, *array.shape)), axis...  8.35 us
    ppermute x2, waiting for transfers between devices, padded_2(): lax.ppermute(head, axis, [((i + 1) % count, i) for i in range(ends)])  7.82 us
    ppermute x2, starting transfers between devices, padded_2(): lax.ppermute(tail, axis, [(i, (i + 1) % count) for i in range(ends)])  7.82 us
    another operation x1, local copies, waits for them, and re-layouts, rescaled_inflow(): return jnp.stack([first_component, second_component, third_component])  6.35 us
    convert_element_type x1, other arithmetic, to_field(): return (math.sqrt(12.0) * scaled).astype(jnp.bfloat16)  3.94 us
    sub x1, other arithmetic, rescaled_inflow(): centred_samples = fluctuation - per_row_means[:, None, None, :]  3.55 us
  transfers between devices with their start and end apart: 5, of which 5 were waited for; matrix products, arithmetic and copies ran while one was open for 0% of the time, Pallas kernels for 0%

commit v1 on v0

v1 whole, which is shorter than its diff:
```python
import functools
import math

import jax
import jax.numpy as jnp
from jax import lax
from jax.experimental import pallas as pl
from jax.experimental.pallas import tpu as pltpu
from jax.sharding import PartitionSpec as P

WMAX = 64
SPANW = 32
TSCALE = 8
STEP = 2
LAG = 3

PAIRS = ((0, 0), (1, 0), (1, 1), (2, 0), (2, 1), (2, 2))
SPREAD_FLOOR = 0.25
INV_RANGE = 1.0 / 1073741824.0
DECAY = math.exp(-math.pi / (2.0 * TSCALE))
FRESH = math.sqrt(1.0 - DECAY * DECAY)
MESH = pl.DeviceIdType.MESH


def raw_taps(offsets, spread):
    inside = jnp.abs(offsets) <= 2.0 * spread
    safe_off = jnp.where(inside, offsets, 0.0)
    return jnp.where(
        inside, jnp.exp(-math.pi * safe_off * safe_off / (8.0 * spread * spread)), 0.0
    )


def wall_bands(widths_ref, raw_ref, own_ref, edge_ref):
    n_rows = widths_ref.shape[1]
    margin = 2 * WMAX
    block = 64
    count = (n_rows + 2 * margin) // block
    spread = widths_ref[...].astype(jnp.float32)

    def fill(i, total):
        at = pl.multiple_of(i * block, block)
        row = lax.broadcasted_iota(jnp.int32, (block, n_rows), 0) + i * block
        col = lax.broadcasted_iota(jnp.int32, (block, n_rows), 1)
        taps = raw_taps((row - margin - col).astype(jnp.float32), spread)
        raw_ref[pl.ds(at, block), :] = taps
        return total + jnp.sum(taps * taps, axis=0, keepdims=True)

    total = lax.fori_loop(0, count, fill, jnp.zeros((1, n_rows), jnp.float32))
    norm = jnp.sqrt(total)
    edge_ref[:margin, :] = (raw_ref[:margin, :] / norm).astype(jnp.bfloat16)
    own_ref[...] = (raw_ref[margin : margin + n_rows, :] / norm).astype(jnp.bfloat16)
    edge_ref[margin:, :] = (raw_ref[margin + n_rows :, :] / norm).astype(jnp.bfloat16)


def span_band(band_ref):
    n_cols, in_count = band_ref.shape
    margin = 2 * SPANW
    row = lax.broadcasted_iota(jnp.int32, (n_cols, in_count), 0)
    col = lax.broadcasted_iota(jnp.int32, (n_cols, in_count), 1)
    taps = raw_taps((col - margin - row).astype(jnp.float32), float(SPANW))
    norm = jnp.sqrt(jnp.sum(taps * taps, axis=1, keepdims=True))
    band_ref[...] = (taps / norm).astype(jnp.bfloat16)


def filter_kernel(
    n_wall, n_span, noise, widths, fluct, totals,
    stage, psi, halo, smooth, from_left, from_right, raw, own_band, edge_band, z_band,
    carry, acc, sums,
    load_sem, wall_send, wall_recv, span_send, span_recv, sum_send, sum_recv,
):
    n_comp, _, n_cols, n_rows = noise.shape
    chunks = stage.shape[0]
    half = n_rows // 2
    rows = n_comp * STEP * n_cols
    w = lax.axis_index("wall")
    p = lax.axis_index("span")
    left, right = lax.rem(p + n_span - 1, n_span), lax.rem(p + 1, n_span)
    below, above = w > 0, w < n_wall - 1

    barrier = pltpu.get_barrier_semaphore()

    def greet(i, _):
        pl.semaphore_signal(
            barrier, inc=1, device_id={"span": lax.rem(p + i, n_span)}, device_id_type=MESH
        )
        return 0

    lax.fori_loop(1, n_span, greet, 0)

    @pl.when(below)
    def _():
        pl.semaphore_signal(barrier, inc=1, device_id={"wall": w - 1}, device_id_type=MESH)

    @pl.when(above)
    def _():
        pl.semaphore_signal(barrier, inc=1, device_id={"wall": w + 1}, device_id_type=MESH)

    def load(k):
        return pltpu.make_async_copy(
            noise.at[:, pl.ds(k * STEP, STEP)], stage.at[k], load_sem.at[k]
        )

    def start_load(k, _):
        load(k).start()
        return 0

    lax.fori_loop(0, chunks, start_load, 0)

    def to_above(k):
        return pltpu.make_async_remote_copy(
            src_ref=psi.at[k, 1], dst_ref=halo.at[k, 0],
            send_sem=wall_send.at[k, 0], recv_sem=wall_recv.at[k, 0],
            device_id={"wall": w + 1}, device_id_type=MESH,
        )

    def to_below(k):
        return pltpu.make_async_remote_copy(
            src_ref=psi.at[k, 0], dst_ref=halo.at[k, 1],
            send_sem=wall_send.at[k, 1], recv_sem=wall_recv.at[k, 1],
            device_id={"wall": w - 1}, device_id_type=MESH,
        )

    def to_right(k):
        return pltpu.make_async_remote_copy(
            src_ref=smooth.at[k], dst_ref=from_left.at[k],
            send_sem=span_send.at[k, 0], recv_sem=span_recv.at[k, 0],
            device_id={"span": right}, device_id_type=MESH,
        )

    def to_left(k):
        return pltpu.make_async_remote_copy(
            src_ref=smooth.at[k], dst_ref=from_right.at[k],
            send_sem=span_send.at[k, 1], recv_sem=span_recv.at[k, 1],
            device_id={"span": left}, device_id_type=MESH,
        )

    def convert(k):
        load(k).wait()
        for c in range(n_comp):
            for s in range(STEP):
                bits = stage[k, c, s].astype(jnp.float32)
                field = (math.sqrt(12.0) * ((bits + 0.5) * INV_RANGE - 0.5)).astype(jnp.bfloat16)
                at = (c * STEP + s) * n_cols
                psi[k, 0, at : at + n_cols, :] = field[:, :half]
                psi[k, 1, at : at + n_cols, :] = field[:, half:]

    def send_wall(k):
        @pl.when(above)
        def _():
            to_above(k).start()

        @pl.when(below)
        def _():
            to_below(k).start()

    convert(0)
    wall_bands(widths, raw, own_band, edge_band)
    span_band(z_band)
    carry[...] = jnp.zeros_like(carry)
    acc[...] = jnp.zeros_like(acc)

    @pl.when(jnp.logical_not(below))
    def _():
        def clear(k, _):
            halo[k, 0] = jnp.zeros(halo.shape[2:], halo.dtype)
            return 0

        lax.fori_loop(0, chunks, clear, 0)

    @pl.when(jnp.logical_not(above))
    def _():
        def clear(k, _):
            halo[k, 1] = jnp.zeros(halo.shape[2:], halo.dtype)
            return 0

        lax.fori_loop(0, chunks, clear, 0)

    pl.semaphore_wait(barrier, n_span - 1 + below.astype(jnp.int32) + above.astype(jnp.int32))

    send_wall(0)

    def convert_and_send(k, _):
        convert(k)
        send_wall(k)
        return 0

    lax.fori_loop(1, chunks, convert_and_send, 0)

    def wall_filter(k):
        @pl.when(below)
        def _():
            to_above(k).wait_recv()

        @pl.when(above)
        def _():
            to_below(k).wait_recv()

        own = jnp.concatenate([psi[k, 0], psi[k, 1]], axis=1)
        edge = jnp.concatenate([halo[k, 0], halo[k, 1]], axis=1)
        filtered = jnp.dot(own, own_band[...], preferred_element_type=jnp.float32) + jnp.dot(
            edge, edge_band[...], preferred_element_type=jnp.float32
        )
        smooth[k] = filtered.astype(jnp.bfloat16).reshape(smooth.shape[1:])
        to_right(k).start()
        to_left(k).start()

    def span_filter(k):
        to_right(k).wait_recv()
        to_left(k).wait_recv()
        for s in range(STEP):
            values = []
            fresh = jnp.where(k * STEP + s == 0, 1.0, FRESH)
            for c in range(n_comp):
                i = c * STEP + s
                window = jnp.concatenate([from_left[k, i], smooth[k, i], from_right[k, i]], axis=0)
                spanned = jnp.dot(z_band[...], window, preferred_element_type=jnp.float32)
                value = DECAY * carry[c] + fresh * spanned
                carry[c] = value
                fluct[c, k * STEP + s] = value
                values.append(value)
            for c in range(n_comp):
                acc[c] += jnp.sum(values[c].reshape(n_cols // 8, 8, n_rows), axis=0)
            for slot, (a, b) in enumerate(PAIRS):
                product = values[a] * values[b]
                acc[n_comp + slot] += jnp.sum(product.reshape(n_cols // 8, 8, n_rows), axis=0)

    def first_steps(k, _):
        wall_filter(k)
        return 0

    def middle_steps(k, _):
        wall_filter(k)
        span_filter(k - LAG)
        return 0

    def last_steps(k, _):
        span_filter(k)
        return 0

    lax.fori_loop(0, LAG, first_steps, 0)
    lax.fori_loop(LAG, chunks, middle_steps, 0)
    lax.fori_loop(chunks - LAG, chunks, last_steps, 0)

    sums[0] = jnp.concatenate(
        [jnp.sum(acc[...], axis=1), jnp.zeros((sums.shape[1] - acc.shape[0], n_rows), jnp.float32)],
        axis=0,
    )

    def share(i):
        return pltpu.make_async_remote_copy(
            src_ref=sums.at[0], dst_ref=sums.at[i],
            send_sem=sum_send.at[i], recv_sem=sum_recv.at[i],
            device_id={"span": lax.rem(p + i, n_span)}, device_id_type=MESH,
        )

    def start_share(i, _):
        share(i).start()
        return 0

    lax.fori_loop(1, n_span, start_share, 0)

    def collect(i, total):
        share(i).wait_recv()
        return total + sums[i]

    totals[...] = lax.fori_loop(1, n_span, collect, sums[0])

    def finish_share(i, _):
        share(i).wait_send()
        return 0

    lax.fori_loop(1, n_span, finish_share, 0)

    def finish_sends(k, _):
        @pl.when(above)
        def _():
            to_above(k).wait_send()

        @pl.when(below)
        def _():
            to_below(k).wait_send()

        to_right(k).wait_send()
        to_left(k).wait_send()
        return 0

    lax.fori_loop(0, chunks, finish_sends, 0)


def lund_transform(sample_covariance, target_factor_diagonal, target_factor_lower):
    cov_00 = sample_covariance[0] + SPREAD_FLOOR
    cov_10 = sample_covariance[1]
    cov_11 = sample_covariance[2] + SPREAD_FLOOR
    cov_20 = sample_covariance[3]
    cov_21 = sample_covariance[4]
    cov_22 = sample_covariance[5] + SPREAD_FLOOR
    chol_00 = jnp.sqrt(cov_00)
    chol_10 = cov_10 / chol_00
    chol_20 = cov_20 / chol_00
    chol_11 = jnp.sqrt(cov_11 - chol_10 * chol_10)
    chol_21 = (cov_21 - chol_20 * chol_10) / chol_11
    chol_22 = jnp.sqrt(cov_22 - chol_20 * chol_20 - chol_21 * chol_21)
    inv_00 = 1.0 / chol_00
    inv_11 = 1.0 / chol_11
    inv_22 = 1.0 / chol_22
    inv_10 = -chol_10 * inv_00 * inv_11
    inv_21 = -chol_21 * inv_11 * inv_22
    inv_20 = -(chol_20 * inv_00 + chol_21 * inv_10) * inv_22
    gain_00 = target_factor_diagonal[0] * inv_00
    gain_10 = target_factor_lower[0] * inv_00 + target_factor_diagonal[1] * inv_10
    gain_11 = target_factor_diagonal[1] * inv_11
    gain_20 = (
        target_factor_lower[1] * inv_00
        + target_factor_lower[2] * inv_10
        + target_factor_diagonal[2] * inv_20
    )
    gain_21 = target_factor_lower[2] * inv_11 + target_factor_diagonal[2] * inv_21
    gain_22 = target_factor_diagonal[2] * inv_22
    return (gain_00,), (gain_10, gain_11), (gain_20, gain_21, gain_22)


def scale_kernel(cell_count, fluct, totals, profile, diagonal, lower, out, gains):
    n_comp, n_step, n_cols, n_rows = fluct.shape

    @pl.when(pl.program_id(0) == 0)
    def _():
        row = [totals[i : i + 1, :] / cell_count for i in range(n_comp + len(PAIRS))]
        means = row[:n_comp]
        spread = [row[n_comp + slot] - means[a] * means[b] for slot, (a, b) in enumerate(PAIRS)]
        factors = lund_transform(
            spread,
            [diagonal[i : i + 1, :] for i in range(3)],
            [lower[i : i + 1, :] for i in range(3)],
        )
        flat = [g for line in factors for g in line]
        for i, value in enumerate(means + flat):
            gains[i] = jnp.broadcast_to(value, (8, n_rows))

    for s in range(n_step):
        centred = [
            fluct[c, s].reshape(n_cols // 8, 8, n_rows) - gains[c] for c in range(n_comp)
        ]
        at = n_comp
        for c in range(n_comp):
            value = profile[c : c + 1, :].reshape(1, 1, n_rows)
            for d in range(c + 1):
                value = value + gains[at] * centred[d]
                at += 1
            out[c, s] = value.reshape(n_cols, n_rows)


def shards(
    noise_bits, filter_widths, target_mean_profile, target_factor_diagonal, target_factor_lower
):
    n_comp, n_samples, n_cols, n_rows = noise_bits.shape
    n_wall, n_span = lax.axis_size("wall"), lax.axis_size("span")
    chunks = n_samples // STEP
    rows = n_comp * STEP * n_cols
    half = n_rows // 2
    bf16, f32 = jnp.bfloat16, jnp.float32
    dma = pltpu.SemaphoreType.DMA
    fluct, totals = pl.pallas_call(
        functools.partial(filter_kernel, n_wall, n_span),
        out_shape=(
            pltpu.VMEM((n_comp, n_samples, n_cols, n_rows), f32),
            pltpu.VMEM((16, n_rows), f32),
        ),
        in_specs=[
            pl.BlockSpec(memory_space=pltpu.HBM),
            pl.BlockSpec(memory_space=pltpu.VMEM),
        ],
        out_specs=(
            pl.BlockSpec(memory_space=pltpu.VMEM),
            pl.BlockSpec(memory_space=pltpu.VMEM),
        ),
        scratch_shapes=[
            pltpu.VMEM((chunks, n_comp, STEP, n_cols, n_rows), jnp.int32),
            pltpu.VMEM((chunks, 2, rows, half), bf16),
            pltpu.VMEM((chunks, 2, rows, half), bf16),
            pltpu.VMEM((chunks, n_comp * STEP, n_cols, n_rows), bf16),
            pltpu.VMEM((chunks, n_comp * STEP, n_cols, n_rows), bf16),
            pltpu.VMEM((chunks, n_comp * STEP, n_cols, n_rows), bf16),
            pltpu.VMEM((n_rows + 4 * WMAX, n_rows), f32),
            pltpu.VMEM((n_rows, n_rows), bf16),
            pltpu.VMEM((4 * WMAX, n_rows), bf16),
            pltpu.VMEM((n_cols, n_cols + 4 * SPANW), bf16),
            pltpu.VMEM((n_comp, n_cols, n_rows), f32),
            pltpu.VMEM((n_comp + len(PAIRS), 8, n_rows), f32),
            pltpu.VMEM((n_span, 16, n_rows), f32),
            dma((chunks,)),
            dma((chunks, 2)),
            dma((chunks, 2)),
            dma((chunks, 2)),
            dma((chunks, 2)),
            dma((n_span,)),
            dma((n_span,)),
        ],
        compiler_params=pltpu.CompilerParams(
            collective_id=0, has_side_effects=True, vmem_limit_bytes=40 * 1024 * 1024
        ),
        name="filters",
    )(
        pltpu.with_memory_space_constraint(noise_bits, pltpu.HBM), filter_widths.reshape(1, n_rows)
    )

    per_step = 2
    block = (n_comp, per_step, n_cols, n_rows)
    whole = lambda *shape: pl.BlockSpec(shape, lambda i: (0,) * len(shape))
    return pl.pallas_call(
        functools.partial(scale_kernel, float(n_samples * n_cols * n_span)),
        grid=(n_samples // per_step,),
        out_shape=jax.ShapeDtypeStruct(noise_bits.shape, f32),
        in_specs=[
            pl.BlockSpec(block, lambda i: (0, i, 0, 0)),
            whole(16, n_rows),
            whole(n_comp, n_rows),
            whole(n_comp, n_rows),
            whole(n_comp, n_rows),
        ],
        out_specs=pl.BlockSpec(block, lambda i: (0, i, 0, 0)),
        scratch_shapes=[pltpu.VMEM((n_comp + len(PAIRS), 8, n_rows), f32)],
        compiler_params=pltpu.CompilerParams(vmem_limit_bytes=16 * 1024 * 1024),
        name="rescale",
    )(fluct, totals, target_mean_profile, target_factor_diagonal, target_factor_lower)


def solution(mesh):
    placed = (
        P(None, None, "span", "wall"),
        P("wall"),
        P(None, "wall"),
        P(None, "wall"),
        P(None, "wall"),
    )
    return jax.shard_map(
        shards, mesh=mesh, in_specs=placed, out_specs=P(None, None, "span", "wall"), check_vma=False
    )
```

time: 129 us -> 67.8 us (0.53)
  the two profiles are of different devices: /device:TPU:97 before, /device:TPU:121 now
where the time goes in v1:
time: 67.8 us; the launch traced here: 67.7 us
  Pallas kernels  66.9 us (99%)
  local copies, waits for them, and re-layouts  0.72 us (1%)
    pallas_call x1, Pallas kernels, shards(): pl.pallas_call(functools.partial(filter_kernel, n_wall, n_span), out_shap...  59.8 us
    pallas_call x1, Pallas kernels, shards(): pl.pallas_call(functools.partial(scale_kernel, float(n_samples * n_cols *...  7.07 us

profile of v1, /device:TPU:121, one launch (start us, length us, event | category | flops | bytes accessed | tf_op | source)
XLA Modules:
  0.0 67.7 jit_solution(12658660738280950996)
XLA Ops:
  0.0 0.0 copy-start.2
  0.0 0.0 copy-start.1
  0.0 0.0 copy-start
  0.0 0.0 copy-start.3
  0.0 0.7 %copy-done.3 = s32[256]{0:T(256)S(1)} copy-done((s32[256]{0:T(256)S(1)}, s32[256]{0:T(256)}, u32[]{:S(2)}) %copy-start.3) | copy-done | bytes 1048
  0.7 59.8 %filters.1 = (f32[3,32,64,256]{3,2,1,0:T(8,128)S(1)}, f32[16,256]{1,0:T(8,128)S(1)}) custom-call(s32[3,32,64,256]{3,2,1,0:T(8,128)} %noise.1, s32[1,256]{1,0:T(1,128)S(1)} %bitcast.1), custom_call_target="tpu_custom_call" | custom-call | tf_op jit(solution)/shard_map/filters/pallas_call | solution.py:362
  60.6 0.0 copy-done.2
  60.6 0.0 copy-done.1
  60.6 0.0 copy-done
  60.6 7.1 %rescale.1 = f32[3,32,64,256]{3,2,1,0:T(8,128)} custom-call(f32[3,32,64,256]{3,2,1,0:T(8,128)S(1)} %get-tuple-element.7.fluct, f32[16,256]{1,0:T(8,128)S(1)} %get-tuple-element.8.totals, f32[3,256]{1,0:T(4,128)S(1)} %copy-done, f32[3,256]{1,0:T(4,128)S(1)} %copy-done.1, f32[3,256]{1,0:T(4,128)S(1)} %copy-done.2), custom_call_target="tpu_custom_call" | custom-call | tf_op jit(solution)/shard_map/rescale/pallas_call | solution.py:409
Async XLA Ops:
  0.0 60.6 %copy-start.2 = (f32[3,256]{1,0:T(4,128)S(1)}, f32[3,256]{1,0:T(4,128)}, u32[]{:S(2)}) copy-start(f32[3,256]{1,0:T(4,128)} %lower.1) | copy-start | bytes 9220
  0.0 60.6 %copy-start.1 = (f32[3,256]{1,0:T(4,128)S(1)}, f32[3,256]{1,0:T(4,128)}, u32[]{:S(2)}) copy-start(f32[3,256]{1,0:T(4,128)} %diagonal.1) | copy-start | bytes 9220
  0.0 60.6 %copy-start = (f32[3,256]{1,0:T(4,128)S(1)}, f32[3,256]{1,0:T(4,128)}, u32[]{:S(2)}) copy-start(f32[3,256]{1,0:T(4,128)} %profile.1) | copy-start | bytes 9220
  0.0 0.7 %copy-start.3 = (s32[256]{0:T(256)S(1)}, s32[256]{0:T(256)}, u32[]{:S(2)}) copy-start(s32[256]{0:T(256)} %param.6) | copy-start | bytes 3076

commit v2 on v1

--- a/solution.py
+++ b/solution.py
@@ -64,14 +64,13 @@
 
 def filter_kernel(
     n_wall, n_span, noise, widths, fluct, totals,
-    stage, psi, halo, smooth, from_left, from_right, raw, own_band, edge_band, z_band,
-    carry, acc, sums,
-    load_sem, wall_send, wall_recv, span_send, span_recv, sum_send, sum_recv,
+    stage, spread, psi, halo, smooth, sides, raw, own_band, edge_band, z_band, carry, acc, sums,
+    load_sem, spread_sem, wall_send, wall_recv, span_send, span_recv, sum_send, sum_recv,
 ):
     n_comp, _, n_cols, n_rows = noise.shape
     chunks = stage.shape[0]
     half = n_rows // 2
-    rows = n_comp * STEP * n_cols
+    moments = acc.shape[0]
     w = lax.axis_index("wall")
     p = lax.axis_index("span")
     left, right = lax.rem(p + n_span - 1, n_span), lax.rem(p + 1, n_span)
@@ -104,35 +103,41 @@
         load(k).start()
         return 0
 
-    lax.fori_loop(0, chunks, start_load, 0)
+    load_spread = pltpu.make_async_copy(widths, spread, spread_sem)
+    load(0).start()
+    load_spread.start()
+    lax.fori_loop(1, chunks, start_load, 0)
 
     def to_above(k):
         return pltpu.make_async_remote_copy(
             src_ref=psi.at[k, 1], dst_ref=halo.at[k, 0],
-            send_sem=wall_send.at[k, 0], recv_sem=wall_recv.at[k, 0],
+            send_sem=wall_send.at[0], recv_sem=wall_recv.at[k],
             device_id={"wall": w + 1}, device_id_type=MESH,
         )
 
     def to_below(k):
         return pltpu.make_async_remote_copy(
             src_ref=psi.at[k, 0], dst_ref=halo.at[k, 1],
-            send_sem=wall_send.at[k, 1], recv_sem=wall_recv.at[k, 1],
+            send_sem=wall_send.at[1], recv_sem=wall_recv.at[k],
             device_id={"wall": w - 1}, device_id_type=MESH,
         )
 
     def to_right(k):
         return pltpu.make_async_remote_copy(
-            src_ref=smooth.at[k], dst_ref=from_left.at[k],
-            send_sem=span_send.at[k, 0], recv_sem=span_recv.at[k, 0],
+            src_ref=smooth.at[k], dst_ref=sides.at[k, 0],
+            send_sem=span_send.at[0], recv_sem=span_recv.at[k],
             device_id={"span": right}, device_id_type=MESH,
         )
 
     def to_left(k):
         return pltpu.make_async_remote_copy(
-            src_ref=smooth.at[k], dst_ref=from_right.at[k],
-            send_sem=span_send.at[k, 1], recv_sem=span_recv.at[k, 1],
+            src_ref=smooth.at[k], dst_ref=sides.at[k, 1],
+            send_sem=span_send.at[1], recv_sem=span_recv.at[k],
             device_id={"span": left}, device_id_type=MESH,
         )
+
+    def landed(ref, sem):
+        pltpu.make_async_copy(ref, ref, sem).wait()
 
     def convert(k):
         load(k).wait()
@@ -153,9 +158,12 @@
         def _():
             to_below(k).start()
 
-    convert(0)
-    wall_bands(widths, raw, own_band, edge_band)
-    span_band(z_band)
+    with jax.named_scope("first_convert"):
+        convert(0)
+    with jax.named_scope("bands"):
+        load_spread.wait()
+        wall_bands(spread, raw, own_band, edge_band)
+        span_band(z_band)
     carry[...] = jnp.zeros_like(carry)
     acc[...] = jnp.zeros_like(acc)
 
@@ -175,7 +183,8 @@
 
         lax.fori_loop(0, chunks, clear, 0)
 
-    pl.semaphore_wait(barrier, n_span - 1 + below.astype(jnp.int32) + above.astype(jnp.int32))
+    with jax.named_scope("greeted"):
+        pl.semaphore_wait(barrier, n_span - 1 + below.astype(jnp.int32) + above.astype(jnp.int32))
 
     send_wall(0)
 
@@ -186,15 +195,22 @@
 
     lax.fori_loop(1, chunks, convert_and_send, 0)
 
+    def wall_arrived(k):
+        @pl.when(jnp.logical_and(below, above))
+        def _():
+            landed(halo.at[k], wall_recv.at[k])
+
+        @pl.when(jnp.logical_not(below))
+        def _():
+            landed(halo.at[k, 1], wall_recv.at[k])
+
+        @pl.when(jnp.logical_not(above))
+        def _():
+            landed(halo.at[k, 0], wall_recv.at[k])
+
     def wall_filter(k):
-        @pl.when(below)
-        def _():
-            to_above(k).wait_recv()
-
-        @pl.when(above)
-        def _():
-            to_below(k).wait_recv()
-
+        with jax.named_scope("wall_wait"):
+            wall_arrived(k)
         own = jnp.concatenate([psi[k, 0], psi[k, 1]], axis=1)
         edge = jnp.concatenate([halo[k, 0], halo[k, 1]], axis=1)
         filtered = jnp.dot(own, own_band[...], preferred_element_type=jnp.float32) + jnp.dot(
@@ -205,14 +221,14 @@
         to_left(k).start()
 
     def span_filter(k):
-        to_right(k).wait_recv()
-        to_left(k).wait_recv()
+        with jax.named_scope("span_wait"):
+            landed(sides.at[k], span_recv.at[k])
         for s in range(STEP):
             values = []
             fresh = jnp.where(k * STEP + s == 0, 1.0, FRESH)
             for c in range(n_comp):
                 i = c * STEP + s
-                window = jnp.concatenate([from_left[k, i], smooth[k, i], from_right[k, i]], axis=0)
+                window = jnp.concatenate([sides[k, 0, i], smooth[k, i], sides[k, 1, i]], axis=0)
                 spanned = jnp.dot(z_band[...], window, preferred_element_type=jnp.float32)
                 value = DECAY * carry[c] + fresh * spanned
                 carry[c] = value
@@ -241,50 +257,42 @@
     lax.fori_loop(LAG, chunks, middle_steps, 0)
     lax.fori_loop(chunks - LAG, chunks, last_steps, 0)
 
-    sums[0] = jnp.concatenate(
-        [jnp.sum(acc[...], axis=1), jnp.zeros((sums.shape[1] - acc.shape[0], n_rows), jnp.float32)],
-        axis=0,
-    )
-
-    def share(i):
-        return pltpu.make_async_remote_copy(
+    for m in range(moments):
+        sums[0, m] = jnp.sum(acc[m], axis=0, keepdims=True)
+
+    def share(i, _):
+        pltpu.make_async_remote_copy(
             src_ref=sums.at[0], dst_ref=sums.at[i],
-            send_sem=sum_send.at[i], recv_sem=sum_recv.at[i],
+            send_sem=sum_send, recv_sem=sum_recv,
             device_id={"span": lax.rem(p + i, n_span)}, device_id_type=MESH,
-        )
-
-    def start_share(i, _):
-        share(i).start()
-        return 0
-
-    lax.fori_loop(1, n_span, start_share, 0)
+        ).start()
+        return 0
+
+    lax.fori_loop(1, n_span, share, 0)
+
+    with jax.named_scope("send_ends"):
+
+        @pl.when(above)
+        def _():
+            landed(psi.at[:, 1], wall_send.at[0])
+
+        @pl.when(below)
+        def _():
+            landed(psi.at[:, 0], wall_send.at[1])
+
+        landed(smooth, span_send.at[0])
+        landed(smooth, span_send.at[1])
+
+    others = sums.at[pl.ds(1, n_span - 1)]
+    with jax.named_scope("sums_wait"):
+        landed(others, sum_recv)
 
     def collect(i, total):
-        share(i).wait_recv()
         return total + sums[i]
 
     totals[...] = lax.fori_loop(1, n_span, collect, sums[0])
-
-    def finish_share(i, _):
-        share(i).wait_send()
-        return 0
-
-    lax.fori_loop(1, n_span, finish_share, 0)
-
-    def finish_sends(k, _):
-        @pl.when(above)
-        def _():
-            to_above(k).wait_send()
-
-        @pl.when(below)
-        def _():
-            to_below(k).wait_send()
-
-        to_right(k).wait_send()
-        to_left(k).wait_send()
-        return 0
-
-    lax.fori_loop(0, chunks, finish_sends, 0)
+    with jax.named_scope("share_ends"):
+        landed(others, sum_send)
 
 
 def lund_transform(sample_covariance, target_factor_diagonal, target_factor_lower):
@@ -319,34 +327,29 @@
     return (gain_00,), (gain_10, gain_11), (gain_20, gain_21, gain_22)
 
 
-def scale_kernel(cell_count, fluct, totals, profile, diagonal, lower, out, gains):
-    n_comp, n_step, n_cols, n_rows = fluct.shape
-
-    @pl.when(pl.program_id(0) == 0)
-    def _():
-        row = [totals[i : i + 1, :] / cell_count for i in range(n_comp + len(PAIRS))]
-        means = row[:n_comp]
-        spread = [row[n_comp + slot] - means[a] * means[b] for slot, (a, b) in enumerate(PAIRS)]
-        factors = lund_transform(
-            spread,
-            [diagonal[i : i + 1, :] for i in range(3)],
-            [lower[i : i + 1, :] for i in range(3)],
-        )
-        flat = [g for line in factors for g in line]
-        for i, value in enumerate(means + flat):
-            gains[i] = jnp.broadcast_to(value, (8, n_rows))
-
-    for s in range(n_step):
-        centred = [
-            fluct[c, s].reshape(n_cols // 8, 8, n_rows) - gains[c] for c in range(n_comp)
-        ]
-        at = n_comp
+def scale_kernel(cell_count, fluct, totals, profile, diagonal, lower, out, ready, sem):
+    n_comp, n_samples, n_cols, n_rows = fluct.shape
+    row = [totals[i] / cell_count for i in range(n_comp + len(PAIRS))]
+    means = row[:n_comp]
+    spread = [row[n_comp + slot] - means[a] * means[b] for slot, (a, b) in enumerate(PAIRS)]
+    factors = lund_transform(
+        spread,
+        [diagonal[i : i + 1, :] for i in range(3)],
+        [lower[i : i + 1, :] for i in range(3)],
+    )
+
+    def one_sample(s, _):
+        centred = [fluct[c, s] - means[c] for c in range(n_comp)]
         for c in range(n_comp):
-            value = profile[c : c + 1, :].reshape(1, 1, n_rows)
+            value = profile[c : c + 1, :]
             for d in range(c + 1):
-                value = value + gains[at] * centred[d]
-                at += 1
-            out[c, s] = value.reshape(n_cols, n_rows)
+                value = value + factors[c][d] * centred[d]
+            ready[c, s] = value
+        pltpu.make_async_copy(ready.at[:, s], out.at[:, s], sem).start()
+        return 0
+
+    lax.fori_loop(0, n_samples, one_sample, 0)
+    pltpu.make_async_copy(ready, out, sem).wait()
 
 
 def shards(
@@ -357,17 +360,18 @@
     chunks = n_samples // STEP
     rows = n_comp * STEP * n_cols
     half = n_rows // 2
+    moments = n_comp + len(PAIRS)
     bf16, f32 = jnp.bfloat16, jnp.float32
     dma = pltpu.SemaphoreType.DMA
     fluct, totals = pl.pallas_call(
         functools.partial(filter_kernel, n_wall, n_span),
         out_shape=(
             pltpu.VMEM((n_comp, n_samples, n_cols, n_rows), f32),
-            pltpu.VMEM((16, n_rows), f32),
+            pltpu.VMEM((moments, 1, n_rows), f32),
         ),
         in_specs=[
             pl.BlockSpec(memory_space=pltpu.HBM),
-            pl.BlockSpec(memory_space=pltpu.VMEM),
+            pl.BlockSpec(memory_space=pltpu.HBM),
         ],
         out_specs=(
             pl.BlockSpec(memory_space=pltpu.VMEM),
@@ -375,50 +379,43 @@
         ),
         scratch_shapes=[
             pltpu.VMEM((chunks, n_comp, STEP, n_cols, n_rows), jnp.int32),
+            pltpu.VMEM((1, n_rows), jnp.int32),
             pltpu.VMEM((chunks, 2, rows, half), bf16),
             pltpu.VMEM((chunks, 2, rows, half), bf16),
             pltpu.VMEM((chunks, n_comp * STEP, n_cols, n_rows), bf16),
-            pltpu.VMEM((chunks, n_comp * STEP, n_cols, n_rows), bf16),
-            pltpu.VMEM((chunks, n_comp * STEP, n_cols, n_rows), bf16),
+            pltpu.VMEM((chunks, 2, n_comp * STEP, n_cols, n_rows), bf16),
             pltpu.VMEM((n_rows + 4 * WMAX, n_rows), f32),
             pltpu.VMEM((n_rows, n_rows), bf16),
             pltpu.VMEM((4 * WMAX, n_rows), bf16),
             pltpu.VMEM((n_cols, n_cols + 4 * SPANW), bf16),
             pltpu.VMEM((n_comp, n_cols, n_rows), f32),
-            pltpu.VMEM((n_comp + len(PAIRS), 8, n_rows), f32),
-            pltpu.VMEM((n_span, 16, n_rows), f32),
+            pltpu.VMEM((moments, 8, n_rows), f32),
+            pltpu.VMEM((n_span, moments, 1, n_rows), f32),
             dma((chunks,)),
-            dma((chunks, 2)),
-            dma((chunks, 2)),
-            dma((chunks, 2)),
-            dma((chunks, 2)),
-            dma((n_span,)),
-            dma((n_span,)),
+            dma,
+            dma((2,)),
+            dma((chunks,)),
+            dma((2,)),
+            dma((chunks,)),
+            dma,
+            dma,
         ],
         compiler_params=pltpu.CompilerParams(
             collective_id=0, has_side_effects=True, vmem_limit_bytes=40 * 1024 * 1024
         ),
         name="filters",
     )(
-        pltpu.with_memory_space_constraint(noise_bits, pltpu.HBM), filter_widths.reshape(1, n_rows)
-    )
-
-    per_step = 2
-    block = (n_comp, per_step, n_cols, n_rows)
-    whole = lambda *shape: pl.BlockSpec(shape, lambda i: (0,) * len(shape))
+        pltpu.with_memory_space_constraint(noise_bits, pltpu.HBM),
+        pltpu.with_memory_space_constraint(filter_widths.reshape(1, n_rows), pltpu.HBM),
+    )
+
+    in_vmem = pl.BlockSpec(memory_space=pltpu.VMEM)
     return pl.pallas_call(
         functools.partial(scale_kernel, float(n_samples * n_cols * n_span)),
-        grid=(n_samples // per_step,),
-        out_shape=jax.ShapeDtypeStruct(noise_bits.shape, f32),
-        in_specs=[
-            pl.BlockSpec(block, lambda i: (0, i, 0, 0)),
-            whole(16, n_rows),
-            whole(n_comp, n_rows),
-            whole(n_comp, n_rows),
-            whole(n_comp, n_rows),
-        ],
-        out_specs=pl.BlockSpec(block, lambda i: (0, i, 0, 0)),
-        scratch_shapes=[pltpu.VMEM((n_comp + len(PAIRS), 8, n_rows), f32)],
+        out_shape=pltpu.HBM(noise_bits.shape, f32),
+        in_specs=[in_vmem] * 5,
+        out_specs=pl.BlockSpec(memory_space=pltpu.HBM),
+        scratch_shapes=[pltpu.VMEM(noise_bits.shape, f32), dma],
         compiler_params=pltpu.CompilerParams(vmem_limit_bytes=16 * 1024 * 1024),
         name="rescale",
     )(fluct, totals, target_mean_profile, target_factor_diagonal, target_factor_lower)

time: 67.8 us -> 58.8 us (0.87)
  the two profiles are of different devices: /device:TPU:121 before, /device:TPU:97 now
where the time goes in v2:
time: 58.8 us; the launch traced here: 58.7 us
  Pallas kernels  58.6 us (100%)
    pallas_call x1, Pallas kernels, shards(): pl.pallas_call(functools.partial(filter_kernel, n_wall, n_span), out_shap...  55.9 us
    pallas_call x1, Pallas kernels, shards(): pl.pallas_call(functools.partial(scale_kernel, float(n_samples * n_cols *...  2.73 us

profile of v2, /device:TPU:97, one launch (start us, length us, event | category | flops | bytes accessed | tf_op | source)
XLA Modules:
  0.0 58.7 jit_solution(14293783887758348078)
XLA Ops:
  0.0 0.0 copy-start.2
  0.0 0.0 copy-start.1
  0.0 0.0 copy-start
  0.0 55.9 %filters.1 = (f32[3,32,64,256]{3,2,1,0:T(8,128)S(1)}, f32[9,1,256]{2,1,0:T(1,128)S(1)}) custom-call(s32[3,32,64,256]{3,2,1,0:T(8,128)} %noise.1, s32[1,256]{1,0:T(1,128)} %bitcast.1), custom_call_target="tpu_custom_call" | custom-call | tf_op jit(solution)/shard_map/filters/pallas_call | solution.py:366
  55.9 0.0 copy-done.2
  55.9 0.0 copy-done.1
  55.9 0.0 copy-done
  55.9 2.7 %rescale.1 = f32[3,32,64,256]{3,2,1,0:T(8,128)} custom-call(f32[3,32,64,256]{3,2,1,0:T(8,128)S(1)} %get-tuple-element.7.fluct, f32[9,1,256]{2,1,0:T(1,128)S(1)} %get-tuple-element.8.totals, f32[3,256]{1,0:T(4,128)S(1)} %copy-done, f32[3,256]{1,0:T(4,128)S(1)} %copy-done.1, f32[3,256]{1,0:T(4,128)S(1)} %copy-done.2), custom_call_target="tpu_custom_call" | custom-call | tf_op jit(solution)/shard_map/rescale/pallas_call | solution.py:413
Async XLA Ops:
  0.0 55.9 %copy-start.2 = (f32[3,256]{1,0:T(4,128)S(1)}, f32[3,256]{1,0:T(4,128)}, u32[]{:S(2)}) copy-start(f32[3,256]{1,0:T(4,128)} %lower.1) | copy-start | bytes 9220
  0.0 55.9 %copy-start.1 = (f32[3,256]{1,0:T(4,128)S(1)}, f32[3,256]{1,0:T(4,128)}, u32[]{:S(2)}) copy-start(f32[3,256]{1,0:T(4,128)} %diagonal.1) | copy-start | bytes 9220
  0.0 55.9 %copy-start = (f32[3,256]{1,0:T(4,128)S(1)}, f32[3,256]{1,0:T(4,128)}, u32[]{:S(2)}) copy-start(f32[3,256]{1,0:T(4,128)} %profile.1) | copy-start | bytes 9220

commit v3 on v2

--- a/solution.py
+++ b/solution.py
@@ -12,7 +12,8 @@
 SPANW = 32
 TSCALE = 8
 STEP = 2
-LAG = 3
+LAG = 4
+FIRST = 3
 
 PAIRS = ((0, 0), (1, 0), (1, 1), (2, 0), (2, 1), (2, 2))
 SPREAD_FLOOR = 0.25
@@ -65,7 +66,7 @@
 def filter_kernel(
     n_wall, n_span, noise, widths, fluct, totals,
     stage, spread, psi, halo, smooth, sides, raw, own_band, edge_band, z_band, carry, acc, sums,
-    load_sem, spread_sem, wall_send, wall_recv, span_send, span_recv, sum_send, sum_recv,
+    load_sem, spread_sem, meet, wall_send, wall_recv, span_send, span_recv, sum_send, sum_recv,
 ):
     n_comp, _, n_cols, n_rows = noise.shape
     chunks = stage.shape[0]
@@ -78,35 +79,47 @@
 
     barrier = pltpu.get_barrier_semaphore()
 
-    def greet(i, _):
-        pl.semaphore_signal(
-            barrier, inc=1, device_id={"span": lax.rem(p + i, n_span)}, device_id_type=MESH
-        )
-        return 0
-
-    lax.fori_loop(1, n_span, greet, 0)
+    def signal(where, **device):
+        pl.semaphore_signal(where, inc=1, device_id=device, device_id_type=MESH)
+
+    signal(barrier, span=left)
+    signal(barrier, span=right)
 
     @pl.when(below)
     def _():
-        pl.semaphore_signal(barrier, inc=1, device_id={"wall": w - 1}, device_id_type=MESH)
+        signal(barrier, wall=w - 1)
 
     @pl.when(above)
     def _():
-        pl.semaphore_signal(barrier, inc=1, device_id={"wall": w + 1}, device_id_type=MESH)
-
-    def load(k):
-        return pltpu.make_async_copy(
-            noise.at[:, pl.ds(k * STEP, STEP)], stage.at[k], load_sem.at[k]
-        )
+        signal(barrier, wall=w + 1)
+
+    rounds = (n_span // 2).bit_length() - 1
+
+    def reach(r):
+        if r < rounds:
+            signal(meet.at[r], span=lax.rem(p + 2**r, n_span))
+            signal(meet.at[r], span=lax.rem(p + n_span - 2**r, n_span))
+
+    def reached(r):
+        if r < rounds:
+            pl.semaphore_wait(meet.at[r], 2)
+
+    n_wall_first = chunks - FIRST
+    order = [k for i in range(FIRST) for k in (n_wall_first + i, i)]
+    late = n_wall_first - FIRST
+
+    def load(k, sem):
+        return pltpu.make_async_copy(noise.at[:, pl.ds(k * STEP, STEP)], stage.at[k], load_sem.at[sem])
 
     def start_load(k, _):
-        load(k).start()
+        load(k, len(order)).start()
         return 0
 
     load_spread = pltpu.make_async_copy(widths, spread, spread_sem)
-    load(0).start()
+    for sem, k in enumerate(order):
+        load(k, sem).start()
     load_spread.start()
-    lax.fori_loop(1, chunks, start_load, 0)
+    lax.fori_loop(FIRST, n_wall_first, start_load, 0)
 
     def to_above(k):
         return pltpu.make_async_remote_copy(
@@ -139,15 +152,17 @@
     def landed(ref, sem):
         pltpu.make_async_copy(ref, ref, sem).wait()
 
-    def convert(k):
-        load(k).wait()
+    def convert(k, span_first):
         for c in range(n_comp):
             for s in range(STEP):
                 bits = stage[k, c, s].astype(jnp.float32)
                 field = (math.sqrt(12.0) * ((bits + 0.5) * INV_RANGE - 0.5)).astype(jnp.bfloat16)
-                at = (c * STEP + s) * n_cols
-                psi[k, 0, at : at + n_cols, :] = field[:, :half]
-                psi[k, 1, at : at + n_cols, :] = field[:, half:]
+                if span_first:
+                    smooth[k, c * STEP + s] = field
+                else:
+                    at = (c * STEP + s) * n_cols
+                    psi[k, 0, at : at + n_cols, :] = field[:, :half]
+                    psi[k, 1, at : at + n_cols, :] = field[:, half:]
 
     def send_wall(k):
         @pl.when(above)
@@ -158,8 +173,31 @@
         def _():
             to_below(k).start()
 
-    with jax.named_scope("first_convert"):
-        convert(0)
+    def send_span(k):
+        to_right(k).start()
+        to_left(k).start()
+
+    for sem, k in enumerate(order):
+        with jax.named_scope("early_convert"):
+            load(k, sem).wait()
+            convert(k, k >= n_wall_first)
+        if k == order[0]:
+            with jax.named_scope("greeted"):
+                pl.semaphore_wait(barrier, 2 + below.astype(jnp.int32) + above.astype(jnp.int32))
+        if k >= n_wall_first:
+            send_span(k)
+        else:
+            send_wall(k)
+
+    def convert_and_send(k, _):
+        convert(k, False)
+        send_wall(k)
+        return 0
+
+    reach(0)
+    with jax.named_scope("converts"):
+        landed(stage.at[pl.ds(FIRST, late)], load_sem.at[len(order)])
+        lax.fori_loop(FIRST, n_wall_first, convert_and_send, 0)
     with jax.named_scope("bands"):
         load_spread.wait()
         wall_bands(spread, raw, own_band, edge_band)
@@ -183,18 +221,6 @@
 
         lax.fori_loop(0, chunks, clear, 0)
 
-    with jax.named_scope("greeted"):
-        pl.semaphore_wait(barrier, n_span - 1 + below.astype(jnp.int32) + above.astype(jnp.int32))
-
-    send_wall(0)
-
-    def convert_and_send(k, _):
-        convert(k)
-        send_wall(k)
-        return 0
-
-    lax.fori_loop(1, chunks, convert_and_send, 0)
-
     def wall_arrived(k):
         @pl.when(jnp.logical_and(below, above))
         def _():
@@ -208,29 +234,42 @@
         def _():
             landed(halo.at[k, 0], wall_recv.at[k])
 
-    def wall_filter(k):
+    def wall_sum(k):
         with jax.named_scope("wall_wait"):
             wall_arrived(k)
         own = jnp.concatenate([psi[k, 0], psi[k, 1]], axis=1)
         edge = jnp.concatenate([halo[k, 0], halo[k, 1]], axis=1)
-        filtered = jnp.dot(own, own_band[...], preferred_element_type=jnp.float32) + jnp.dot(
+        total = jnp.dot(own, own_band[...], preferred_element_type=jnp.float32) + jnp.dot(
             edge, edge_band[...], preferred_element_type=jnp.float32
         )
-        smooth[k] = filtered.astype(jnp.bfloat16).reshape(smooth.shape[1:])
-        to_right(k).start()
-        to_left(k).start()
-
-    def span_filter(k):
+        return total.reshape(n_comp * STEP, n_cols, n_rows)
+
+    def span_arrived(k):
         with jax.named_scope("span_wait"):
             landed(sides.at[k], span_recv.at[k])
+
+    def span_sum(k, i):
+        window = jnp.concatenate([sides[k, 0, i], smooth[k, i], sides[k, 1, i]], axis=0)
+        return jnp.dot(z_band[...], window, preferred_element_type=jnp.float32)
+
+    def wall_filter(k):
+        smooth[k] = wall_sum(k).astype(jnp.bfloat16)
+        send_span(k)
+
+    def span_filter_first(k):
+        span_arrived(k)
+        for i in range(n_comp * STEP):
+            field = span_sum(k, i).astype(jnp.bfloat16)
+            psi[k, 0, i * n_cols : (i + 1) * n_cols, :] = field[:, :half]
+            psi[k, 1, i * n_cols : (i + 1) * n_cols, :] = field[:, half:]
+        send_wall(k)
+
+    def advance(k, filtered):
         for s in range(STEP):
+            fresh = jnp.where(k * STEP + s == 0, 1.0, FRESH)
             values = []
-            fresh = jnp.where(k * STEP + s == 0, 1.0, FRESH)
             for c in range(n_comp):
-                i = c * STEP + s
-                window = jnp.concatenate([sides[k, 0, i], smooth[k, i], sides[k, 1, i]], axis=0)
-                spanned = jnp.dot(z_band[...], window, preferred_element_type=jnp.float32)
-                value = DECAY * carry[c] + fresh * spanned
+                value = DECAY * carry[c] + fresh * filtered(c, s)
                 carry[c] = value
                 fluct[c, k * STEP + s] = value
                 values.append(value)
@@ -240,9 +279,15 @@
                 product = values[a] * values[b]
                 acc[n_comp + slot] += jnp.sum(product.reshape(n_cols // 8, 8, n_rows), axis=0)
 
-    def first_steps(k, _):
-        wall_filter(k)
-        return 0
+    def span_filter(k):
+        span_arrived(k)
+        advance(k, lambda c, s: span_sum(k, c * STEP + s))
+
+    def wall_filter_last(k):
+        fields = wall_sum(k)
+        for c in range(n_comp):
+            for s in range(STEP):
+                fluct[c, k * STEP + s] = fields[c * STEP + s]
 
     def middle_steps(k, _):
         wall_filter(k)
@@ -253,22 +298,43 @@
         span_filter(k)
         return 0
 
-    lax.fori_loop(0, LAG, first_steps, 0)
-    lax.fori_loop(LAG, chunks, middle_steps, 0)
-    lax.fori_loop(chunks - LAG, chunks, last_steps, 0)
-
+    for k in range(LAG):
+        wall_filter(k)
+        if k < FIRST:
+            span_filter_first(n_wall_first + k)
+        reached(k)
+        reach(k + 1)
+    lax.fori_loop(LAG, n_wall_first, middle_steps, 0)
+    for r in range(LAG, rounds):
+        reached(r)
+        reach(r + 1)
+    lax.fori_loop(n_wall_first - LAG, n_wall_first - 1, last_steps, 0)
+    for k in range(n_wall_first, chunks):
+        wall_filter_last(k)
+    span_filter(n_wall_first - 1)
+    for k in range(n_wall_first, chunks):
+        advance(k, lambda c, s: fluct[c, k * STEP + s])
     for m in range(moments):
         sums[0, m] = jnp.sum(acc[m], axis=0, keepdims=True)
 
-    def share(i, _):
-        pltpu.make_async_remote_copy(
-            src_ref=sums.at[0], dst_ref=sums.at[i],
-            send_sem=sum_send, recv_sem=sum_recv,
-            device_id={"span": lax.rem(p + i, n_span)}, device_id_type=MESH,
-        ).start()
-        return 0
-
-    lax.fori_loop(1, n_span, share, 0)
+    n_y = min(4, n_span // 2)
+    n_x = n_span // (2 * n_y)
+    x, y, core = p // (2 * n_y), lax.rem(p // 2, n_y), lax.rem(p, 2)
+
+    def hops(step):
+        return min(step[0], n_x - step[0]) + min(step[1], n_y - step[1])
+
+    steps = [(dx, dy, dc) for dx in range(n_x) for dy in range(n_y) for dc in range(2)]
+    steps.sort(key=hops)
+    with jax.named_scope("share"):
+        for i in reversed(range(1, n_span)):
+            dx, dy, dc = steps[i]
+            there = (lax.rem(x + dx, n_x) * n_y + lax.rem(y + dy, n_y)) * 2 + lax.rem(core + dc, 2)
+            pltpu.make_async_remote_copy(
+                src_ref=sums.at[0], dst_ref=sums.at[i],
+                send_sem=sum_send, recv_sem=sum_recv,
+                device_id={"span": there}, device_id_type=MESH,
+            ).start()
 
     with jax.named_scope("send_ends"):
 
@@ -391,8 +457,9 @@
             pltpu.VMEM((n_comp, n_cols, n_rows), f32),
             pltpu.VMEM((moments, 8, n_rows), f32),
             pltpu.VMEM((n_span, moments, 1, n_rows), f32),
-            dma((chunks,)),
+            dma((2 * FIRST + 1,)),
             dma,
+            pltpu.SemaphoreType.REGULAR((max(1, (n_span // 2).bit_length() - 1),)),
             dma((2,)),
             dma((chunks,)),
             dma((2,)),

time: 58.8 us -> 53.1 us (0.903)
  Pallas kernels: 58.6 us -> 53 us
    pallas_call x1, Pallas kernels: 55.9 us -> 50.2 us  [shards(): pl.pallas_call(functools.partial(filter_kernel, n_wall, n_span), out_shap...]
where the time goes in v3:
time: 53.1 us; the launch traced here: 53 us
  Pallas kernels  53 us (100%)
    pallas_call x1, Pallas kernels, shards(): pl.pallas_call(functools.partial(filter_kernel, n_wall, n_span), out_shap...  50.2 us
    pallas_call x1, Pallas kernels, shards(): pl.pallas_call(functools.partial(scale_kernel, float(n_samples * n_cols *...  2.73 us

profile of v3, /device:TPU:97, one launch (start us, length us, event | category | flops | bytes accessed | tf_op | source)
XLA Modules:
  0.0 53.0 jit_solution(15975629781182035030)
XLA Ops:
  0.0 0.0 copy-start.2
  0.0 0.0 copy-start.1
  0.0 0.0 copy-start
  0.0 50.2 %filters.1 = (f32[3,32,64,256]{3,2,1,0:T(8,128)S(1)}, f32[9,1,256]{2,1,0:T(1,128)S(1)}) custom-call(s32[3,32,64,256]{3,2,1,0:T(8,128)} %noise.1, s32[1,256]{1,0:T(1,128)} %bitcast.1), custom_call_target="tpu_custom_call" | custom-call | tf_op jit(solution)/shard_map/filters/pallas_call | solution.py:432
  50.3 0.0 copy-done.2
  50.3 0.0 copy-done.1
  50.3 0.0 copy-done
  50.3 2.7 %rescale.1 = f32[3,32,64,256]{3,2,1,0:T(8,128)} custom-call(f32[3,32,64,256]{3,2,1,0:T(8,128)S(1)} %get-tuple-element.7.fluct, f32[9,1,256]{2,1,0:T(1,128)S(1)} %get-tuple-element.8.totals, f32[3,256]{1,0:T(4,128)S(1)} %copy-done, f32[3,256]{1,0:T(4,128)S(1)} %copy-done.1, f32[3,256]{1,0:T(4,128)S(1)} %copy-done.2), custom_call_target="tpu_custom_call" | custom-call | tf_op jit(solution)/shard_map/rescale/pallas_call | solution.py:480
Async XLA Ops:
  0.0 50.3 %copy-start.2 = (f32[3,256]{1,0:T(4,128)S(1)}, f32[3,256]{1,0:T(4,128)}, u32[]{:S(2)}) copy-start(f32[3,256]{1,0:T(4,128)} %lower.1) | copy-start | bytes 9220
  0.0 50.3 %copy-start.1 = (f32[3,256]{1,0:T(4,128)S(1)}, f32[3,256]{1,0:T(4,128)}, u32[]{:S(2)}) copy-start(f32[3,256]{1,0:T(4,128)} %diagonal.1) | copy-start | bytes 9220
  0.0 50.3 %copy-start = (f32[3,256]{1,0:T(4,128)S(1)}, f32[3,256]{1,0:T(4,128)}, u32[]{:S(2)}) copy-start(f32[3,256]{1,0:T(4,128)} %profile.1) | copy-start | bytes 9220

commit v4 on v3

--- a/solution.py
+++ b/solution.py
@@ -12,8 +12,8 @@
 SPANW = 32
 TSCALE = 8
 STEP = 2
-LAG = 4
-FIRST = 3
+LAG = 5
+FIRST = 4
 
 PAIRS = ((0, 0), (1, 0), (1, 1), (2, 0), (2, 1), (2, 2))
 SPREAD_FLOOR = 0.25
@@ -79,6 +79,30 @@
 
     barrier = pltpu.get_barrier_semaphore()
 
+    n_wall_first = chunks - FIRST
+    plain = n_wall_first - FIRST
+    early = [k for i in range(FIRST) for k in (n_wall_first + i, i)]
+
+    def time_of(k):
+        if isinstance(k, int) and k >= n_wall_first:
+            return plain + 1 + 2 * (k - n_wall_first)
+        return k + (k // plain) * (k - plain)
+
+    def load(k, sem):
+        return pltpu.make_async_copy(
+            noise.at[:, pl.ds(time_of(k) * STEP, STEP)], stage.at[k], load_sem.at[sem]
+        )
+
+    def start_load(k, _):
+        load(k, len(early)).start()
+        return 0
+
+    load_spread = pltpu.make_async_copy(widths, spread, spread_sem)
+    for sem, k in enumerate(early):
+        load(k, sem).start()
+    load_spread.start()
+    lax.fori_loop(FIRST, n_wall_first, start_load, 0)
+
     def signal(where, **device):
         pl.semaphore_signal(where, inc=1, device_id=device, device_id_type=MESH)
 
@@ -103,23 +127,6 @@
     def reached(r):
         if r < rounds:
             pl.semaphore_wait(meet.at[r], 2)
-
-    n_wall_first = chunks - FIRST
-    order = [k for i in range(FIRST) for k in (n_wall_first + i, i)]
-    late = n_wall_first - FIRST
-
-    def load(k, sem):
-        return pltpu.make_async_copy(noise.at[:, pl.ds(k * STEP, STEP)], stage.at[k], load_sem.at[sem])
-
-    def start_load(k, _):
-        load(k, len(order)).start()
-        return 0
-
-    load_spread = pltpu.make_async_copy(widths, spread, spread_sem)
-    for sem, k in enumerate(order):
-        load(k, sem).start()
-    load_spread.start()
-    lax.fori_loop(FIRST, n_wall_first, start_load, 0)
 
     def to_above(k):
         return pltpu.make_async_remote_copy(
@@ -177,11 +184,11 @@
         to_right(k).start()
         to_left(k).start()
 
-    for sem, k in enumerate(order):
+    for sem, k in enumerate(early):
         with jax.named_scope("early_convert"):
             load(k, sem).wait()
             convert(k, k >= n_wall_first)
-        if k == order[0]:
+        if sem == 0:
             with jax.named_scope("greeted"):
                 pl.semaphore_wait(barrier, 2 + below.astype(jnp.int32) + above.astype(jnp.int32))
         if k >= n_wall_first:
@@ -196,7 +203,7 @@
 
     reach(0)
     with jax.named_scope("converts"):
-        landed(stage.at[pl.ds(FIRST, late)], load_sem.at[len(order)])
+        landed(stage.at[pl.ds(FIRST, plain)], load_sem.at[len(early)])
         lax.fori_loop(FIRST, n_wall_first, convert_and_send, 0)
     with jax.named_scope("bands"):
         load_spread.wait()
@@ -266,12 +273,13 @@
 
     def advance(k, filtered):
         for s in range(STEP):
-            fresh = jnp.where(k * STEP + s == 0, 1.0, FRESH)
+            t = time_of(k) * STEP + s
+            fresh = jnp.where(t == 0, 1.0, FRESH)
             values = []
             for c in range(n_comp):
                 value = DECAY * carry[c] + fresh * filtered(c, s)
                 carry[c] = value
-                fluct[c, k * STEP + s] = value
+                fluct[c, t] = value
                 values.append(value)
             for c in range(n_comp):
                 acc[c] += jnp.sum(values[c].reshape(n_cols // 8, 8, n_rows), axis=0)
@@ -287,7 +295,7 @@
         fields = wall_sum(k)
         for c in range(n_comp):
             for s in range(STEP):
-                fluct[c, k * STEP + s] = fields[c * STEP + s]
+                fluct[c, time_of(k) * STEP + s] = fields[c * STEP + s]
 
     def middle_steps(k, _):
         wall_filter(k)
@@ -308,33 +316,30 @@
     for r in range(LAG, rounds):
         reached(r)
         reach(r + 1)
-    lax.fori_loop(n_wall_first - LAG, n_wall_first - 1, last_steps, 0)
-    for k in range(n_wall_first, chunks):
-        wall_filter_last(k)
-    span_filter(n_wall_first - 1)
-    for k in range(n_wall_first, chunks):
-        advance(k, lambda c, s: fluct[c, k * STEP + s])
+    lax.fori_loop(n_wall_first - LAG, plain, last_steps, 0)
+    for i in range(FIRST):
+        wall_filter_last(n_wall_first + i)
+        span_filter(plain + i)
+        advance(n_wall_first + i, lambda c, s: fluct[c, time_of(n_wall_first + i) * STEP + s])
+
     for m in range(moments):
-        sums[0, m] = jnp.sum(acc[m], axis=0, keepdims=True)
+        sums[p, m] = jnp.sum(acc[m], axis=0, keepdims=True)
 
     n_y = min(4, n_span // 2)
-    n_x = n_span // (2 * n_y)
-    x, y, core = p // (2 * n_y), lax.rem(p // 2, n_y), lax.rem(p, 2)
-
-    def hops(step):
-        return min(step[0], n_x - step[0]) + min(step[1], n_y - step[1])
-
-    steps = [(dx, dy, dc) for dx in range(n_x) for dy in range(n_y) for dc in range(2)]
-    steps.sort(key=hops)
+
+    def rank(there):
+        return there // (2 * n_y) + there // 2 % n_y
+
     with jax.named_scope("share"):
-        for i in reversed(range(1, n_span)):
-            dx, dy, dc = steps[i]
-            there = (lax.rem(x + dx, n_x) * n_y + lax.rem(y + dy, n_y)) * 2 + lax.rem(core + dc, 2)
-            pltpu.make_async_remote_copy(
-                src_ref=sums.at[0], dst_ref=sums.at[i],
-                send_sem=sum_send, recv_sem=sum_recv,
-                device_id={"span": there}, device_id_type=MESH,
-            ).start()
+        for there in sorted(range(n_span), key=rank):
+
+            @pl.when(p != there)
+            def _():
+                pltpu.make_async_remote_copy(
+                    src_ref=sums.at[p], dst_ref=sums.at[p],
+                    send_sem=sum_send, recv_sem=sum_recv,
+                    device_id={"span": there}, device_id_type=MESH,
+                ).start()
 
     with jax.named_scope("send_ends"):
 
@@ -395,7 +400,8 @@
 
 def scale_kernel(cell_count, fluct, totals, profile, diagonal, lower, out, ready, sem):
     n_comp, n_samples, n_cols, n_rows = fluct.shape
-    row = [totals[i] / cell_count for i in range(n_comp + len(PAIRS))]
+    moments = n_comp + len(PAIRS)
+    row = [totals[i] / cell_count for i in range(moments)]
     means = row[:n_comp]
     spread = [row[n_comp + slot] - means[a] * means[b] for slot, (a, b) in enumerate(PAIRS)]
     factors = lund_transform(

time: 53.1 us -> 52 us (0.979)
  Pallas kernels: 53 us -> 51.9 us
    pallas_call x1, Pallas kernels: 50.2 us -> 49.2 us  [shards(): pl.pallas_call(functools.partial(filter_kernel, n_wall, n_span), out_shap...]
where the time goes in v4:
time: 52 us
  Pallas kernels  51.9 us (100%)
    pallas_call x1, Pallas kernels, shards(): pl.pallas_call(functools.partial(filter_kernel, n_wall, n_span), out_shap...  49.2 us
    pallas_call x1, Pallas kernels, shards(): pl.pallas_call(functools.partial(scale_kernel, float(n_samples * n_cols *...  2.73 us

profile of v4, /device:TPU:97, one launch (start us, length us, event | category | flops | bytes accessed | tf_op | source)
XLA Modules:
  0.0 52.0 jit_solution(12929019355528303215)
XLA Ops:
  0.0 0.0 copy-start.2
  0.0 0.0 copy-start.1
  0.0 0.0 copy-start
  0.0 49.2 %filters.1 = (f32[3,32,64,256]{3,2,1,0:T(8,128)S(1)}, f32[9,1,256]{2,1,0:T(1,128)S(1)}) custom-call(s32[3,32,64,256]{3,2,1,0:T(8,128)} %noise.1, s32[1,256]{1,0:T(1,128)} %bitcast.1), custom_call_target="tpu_custom_call" | custom-call | tf_op jit(solution)/shard_map/filters/pallas_call | solution.py:438
  49.2 0.0 copy-done.2
  49.2 0.0 copy-done.1
  49.2 0.0 copy-done
  49.2 2.7 %rescale.1 = f32[3,32,64,256]{3,2,1,0:T(8,128)} custom-call(f32[3,32,64,256]{3,2,1,0:T(8,128)S(1)} %get-tuple-element.7.fluct, f32[9,1,256]{2,1,0:T(1,128)S(1)} %get-tuple-element.8.totals, f32[3,256]{1,0:T(4,128)S(1)} %copy-done, f32[3,256]{1,0:T(4,128)S(1)} %copy-done.1, f32[3,256]{1,0:T(4,128)S(1)} %copy-done.2), custom_call_target="tpu_custom_call" | custom-call | tf_op jit(solution)/shard_map/rescale/pallas_call | solution.py:486
Async XLA Ops:
  0.0 49.2 %copy-start.2 = (f32[3,256]{1,0:T(4,128)S(1)}, f32[3,256]{1,0:T(4,128)}, u32[]{:S(2)}) copy-start(f32[3,256]{1,0:T(4,128)} %lower.1) | copy-start | bytes 9220
  0.0 49.2 %copy-start.1 = (f32[3,256]{1,0:T(4,128)S(1)}, f32[3,256]{1,0:T(4,128)}, u32[]{:S(2)}) copy-start(f32[3,256]{1,0:T(4,128)} %diagonal.1) | copy-start | bytes 9220
  0.0 49.2 %copy-start = (f32[3,256]{1,0:T(4,128)S(1)}, f32[3,256]{1,0:T(4,128)}, u32[]{:S(2)}) copy-start(f32[3,256]{1,0:T(4,128)} %profile.1) | copy-start | bytes 9220

commit v5 on v4

--- a/solution.py
+++ b/solution.py
@@ -79,6 +79,20 @@
 
     barrier = pltpu.get_barrier_semaphore()
 
+    def signal(where, **device):
+        pl.semaphore_signal(where, inc=1, device_id=device, device_id_type=MESH)
+
+    signal(barrier, span=left)
+    signal(barrier, span=right)
+
+    @pl.when(below)
+    def _():
+        signal(barrier, wall=w - 1)
+
+    @pl.when(above)
+    def _():
+        signal(barrier, wall=w + 1)
+
     n_wall_first = chunks - FIRST
     plain = n_wall_first - FIRST
     early = [k for i in range(FIRST) for k in (n_wall_first + i, i)]
@@ -102,20 +116,6 @@
         load(k, sem).start()
     load_spread.start()
     lax.fori_loop(FIRST, n_wall_first, start_load, 0)
-
-    def signal(where, **device):
-        pl.semaphore_signal(where, inc=1, device_id=device, device_id_type=MESH)
-
-    signal(barrier, span=left)
-    signal(barrier, span=right)
-
-    @pl.when(below)
-    def _():
-        signal(barrier, wall=w - 1)
-
-    @pl.when(above)
-    def _():
-        signal(barrier, wall=w + 1)
 
     rounds = (n_span // 2).bit_length() - 1
 
@@ -327,8 +327,12 @@
 
     n_y = min(4, n_span // 2)
 
+    n_x = n_span // (2 * n_y)
+    in_group = 2 * n_y
+    group = p // in_group
+
     def rank(there):
-        return there // (2 * n_y) + there // 2 % n_y
+        return there // in_group + there // 2 % n_y
 
     with jax.named_scope("share"):
         for there in sorted(range(n_span), key=rank):
@@ -337,7 +341,7 @@
             def _():
                 pltpu.make_async_remote_copy(
                     src_ref=sums.at[p], dst_ref=sums.at[p],
-                    send_sem=sum_send, recv_sem=sum_recv,
+                    send_sem=sum_send, recv_sem=sum_recv.at[group],
                     device_id={"span": there}, device_id_type=MESH,
                 ).start()
 
@@ -354,16 +358,25 @@
         landed(smooth, span_send.at[0])
         landed(smooth, span_send.at[1])
 
-    others = sums.at[pl.ds(1, n_span - 1)]
-    with jax.named_scope("sums_wait"):
-        landed(others, sum_recv)
-
     def collect(i, total):
         return total + sums[i]
 
-    totals[...] = lax.fori_loop(1, n_span, collect, sums[0])
+    total = jnp.zeros(sums.shape[1:], jnp.float32)
+    with jax.named_scope("sums_wait"):
+        for g in range(n_x):
+
+            @pl.when(group == g)
+            def _():
+                landed(sums.at[pl.ds(0, in_group - 1)], sum_recv.at[g])
+
+            @pl.when(group != g)
+            def _():
+                landed(sums.at[pl.ds(0, in_group)], sum_recv.at[g])
+
+            total = lax.fori_loop(g * in_group, (g + 1) * in_group, collect, total)
+    totals[...] = total
     with jax.named_scope("share_ends"):
-        landed(others, sum_send)
+        landed(sums.at[pl.ds(0, n_span - 1)], sum_send)
 
 
 def lund_transform(sample_covariance, target_factor_diagonal, target_factor_lower):
@@ -373,15 +386,12 @@
     cov_20 = sample_covariance[3]
     cov_21 = sample_covariance[4]
     cov_22 = sample_covariance[5] + SPREAD_FLOOR
-    chol_00 = jnp.sqrt(cov_00)
-    chol_10 = cov_10 / chol_00
-    chol_20 = cov_20 / chol_00
-    chol_11 = jnp.sqrt(cov_11 - chol_10 * chol_10)
-    chol_21 = (cov_21 - chol_20 * chol_10) / chol_11
-    chol_22 = jnp.sqrt(cov_22 - chol_20 * chol_20 - chol_21 * chol_21)
-    inv_00 = 1.0 / chol_00
-    inv_11 = 1.0 / chol_11
-    inv_22 = 1.0 / chol_22
+    inv_00 = lax.rsqrt(cov_00)
+    chol_10 = cov_10 * inv_00
+    chol_20 = cov_20 * inv_00
+    inv_11 = lax.rsqrt(cov_11 - chol_10 * chol_10)
+    chol_21 = (cov_21 - chol_20 * chol_10) * inv_11
+    inv_22 = lax.rsqrt(cov_22 - chol_20 * chol_20 - chol_21 * chol_21)
     inv_10 = -chol_10 * inv_00 * inv_11
     inv_21 = -chol_21 * inv_11 * inv_22
     inv_20 = -(chol_20 * inv_00 + chol_21 * inv_10) * inv_22
@@ -401,7 +411,7 @@
 def scale_kernel(cell_count, fluct, totals, profile, diagonal, lower, out, ready, sem):
     n_comp, n_samples, n_cols, n_rows = fluct.shape
     moments = n_comp + len(PAIRS)
-    row = [totals[i] / cell_count for i in range(moments)]
+    row = [totals[i] * (1.0 / cell_count) for i in range(moments)]
     means = row[:n_comp]
     spread = [row[n_comp + slot] - means[a] * means[b] for slot, (a, b) in enumerate(PAIRS)]
     factors = lund_transform(
@@ -471,7 +481,7 @@
             dma((2,)),
             dma((chunks,)),
             dma,
-            dma,
+            dma((4,)),
         ],
         compiler_params=pltpu.CompilerParams(
             collective_id=0, has_side_effects=True, vmem_limit_bytes=40 * 1024 * 1024

time: 52 us -> 51.7 us (level)
  no operation moved by 1% of the time
where the time goes in v5:
time: 51.7 us
  Pallas kernels  51.6 us (100%)
    pallas_call x1, Pallas kernels, shards(): pl.pallas_call(functools.partial(filter_kernel, n_wall, n_span), out_shap...  48.9 us
    pallas_call x1, Pallas kernels, shards(): pl.pallas_call(functools.partial(scale_kernel, float(n_samples * n_cols *...  2.7 us

profile of v5, /device:TPU:97, one launch (start us, length us, event | category | flops | bytes accessed | tf_op | source)
XLA Modules:
  0.0 51.7 jit_solution(6901629152151896900)
XLA Ops:
  0.0 0.0 copy-start.2
  0.0 0.0 copy-start.1
  0.0 0.0 copy-start
  0.0 48.9 %filters.1 = (f32[3,32,64,256]{3,2,1,0:T(8,128)S(1)}, f32[9,1,256]{2,1,0:T(1,128)S(1)}) custom-call(s32[3,32,64,256]{3,2,1,0:T(8,128)} %noise.1, s32[1,256]{1,0:T(1,128)} %bitcast.1), custom_call_target="tpu_custom_call" | custom-call | tf_op jit(solution)/shard_map/filters/pallas_call | solution.py:448
  48.9 0.0 copy-done.2
  48.9 0.0 copy-done.1
  49.0 0.0 copy-done
  49.0 2.7 %rescale.1 = f32[3,32,64,256]{3,2,1,0:T(8,128)} custom-call(f32[3,32,64,256]{3,2,1,0:T(8,128)S(1)} %get-tuple-element.7.fluct, f32[9,1,256]{2,1,0:T(1,128)S(1)} %get-tuple-element.8.totals, f32[3,256]{1,0:T(4,128)S(1)} %copy-done, f32[3,256]{1,0:T(4,128)S(1)} %copy-done.1, f32[3,256]{1,0:T(4,128)S(1)} %copy-done.2), custom_call_target="tpu_custom_call" | custom-call | tf_op jit(solution)/shard_map/rescale/pallas_call | solution.py:496
Async XLA Ops:
  0.0 48.9 %copy-start.2 = (f32[3,256]{1,0:T(4,128)S(1)}, f32[3,256]{1,0:T(4,128)}, u32[]{:S(2)}) copy-start(f32[3,256]{1,0:T(4,128)} %lower.1) | copy-start | bytes 9220
  0.0 48.9 %copy-start.1 = (f32[3,256]{1,0:T(4,128)S(1)}, f32[3,256]{1,0:T(4,128)}, u32[]{:S(2)}) copy-start(f32[3,256]{1,0:T(4,128)} %diagonal.1) | copy-start | bytes 9220
  0.0 49.0 %copy-start = (f32[3,256]{1,0:T(4,128)S(1)}, f32[3,256]{1,0:T(4,128)}, u32[]{:S(2)}) copy-start(f32[3,256]{1,0:T(4,128)} %profile.1) | copy-start | bytes 9220

commit v6 on v5

--- a/solution.py
+++ b/solution.py
@@ -65,10 +65,10 @@
 
 def filter_kernel(
     n_wall, n_span, noise, widths, fluct, totals,
-    stage, spread, psi, halo, smooth, sides, raw, own_band, edge_band, z_band, carry, acc, sums,
+    stage, spread, psi, halo, smooth, sides, raw, own_band, edge_band, z_band, acc, sums,
     load_sem, spread_sem, meet, wall_send, wall_recv, span_send, span_recv, sum_send, sum_recv,
 ):
-    n_comp, _, n_cols, n_rows = noise.shape
+    n_comp, n_samples, n_cols, n_rows = noise.shape
     chunks = stage.shape[0]
     half = n_rows // 2
     moments = acc.shape[0]
@@ -209,7 +209,6 @@
         load_spread.wait()
         wall_bands(spread, raw, own_band, edge_band)
         span_band(z_band)
-    carry[...] = jnp.zeros_like(carry)
     acc[...] = jnp.zeros_like(acc)
 
     @pl.when(jnp.logical_not(below))
@@ -277,8 +276,9 @@
             fresh = jnp.where(t == 0, 1.0, FRESH)
             values = []
             for c in range(n_comp):
-                value = DECAY * carry[c] + fresh * filtered(c, s)
-                carry[c] = value
+                earlier = fluct[c, lax.rem(t + n_samples - 1, n_samples)]
+                kept = jnp.where(t == 0, 0.0, DECAY * earlier)
+                value = kept + fresh * filtered(c, s)
                 fluct[c, t] = value
                 values.append(value)
             for c in range(n_comp):
@@ -470,7 +470,6 @@
             pltpu.VMEM((n_rows, n_rows), bf16),
             pltpu.VMEM((4 * WMAX, n_rows), bf16),
             pltpu.VMEM((n_cols, n_cols + 4 * SPANW), bf16),
-            pltpu.VMEM((n_comp, n_cols, n_rows), f32),
             pltpu.VMEM((moments, 8, n_rows), f32),
             pltpu.VMEM((n_span, moments, 1, n_rows), f32),
             dma((2 * FIRST + 1,)),

time: 51.7 us -> 51.7 us (level)
  no operation moved by 1% of the time
where the time goes in v6:
time: 51.7 us
  Pallas kernels  51.6 us (100%)
    pallas_call x1, Pallas kernels, shards(): pl.pallas_call(functools.partial(filter_kernel, n_wall, n_span), out_shap...  48.9 us
    pallas_call x1, Pallas kernels, shards(): pl.pallas_call(functools.partial(scale_kernel, float(n_samples * n_cols *...  2.7 us

profile of v6, /device:TPU:97, one launch (start us, length us, event | category | flops | bytes accessed | tf_op | source)
XLA Modules:
  0.0 51.7 jit_solution(14164853416543125146)
XLA Ops:
  0.0 0.0 copy-start.2
  0.0 0.0 copy-start.1
  0.0 0.0 copy-start
  0.0 48.9 %filters.1 = (f32[3,32,64,256]{3,2,1,0:T(8,128)S(1)}, f32[9,1,256]{2,1,0:T(1,128)S(1)}) custom-call(s32[3,32,64,256]{3,2,1,0:T(8,128)} %noise.1, s32[1,256]{1,0:T(1,128)} %bitcast.1), custom_call_target="tpu_custom_call" | custom-call | tf_op jit(solution)/shard_map/filters/pallas_call | solution.py:448
  48.9 0.0 copy-done.2
  48.9 0.0 copy-done.1
  49.0 0.0 copy-done
  49.0 2.7 %rescale.1 = f32[3,32,64,256]{3,2,1,0:T(8,128)} custom-call(f32[3,32,64,256]{3,2,1,0:T(8,128)S(1)} %get-tuple-element.7.fluct, f32[9,1,256]{2,1,0:T(1,128)S(1)} %get-tuple-element.8.totals, f32[3,256]{1,0:T(4,128)S(1)} %copy-done, f32[3,256]{1,0:T(4,128)S(1)} %copy-done.1, f32[3,256]{1,0:T(4,128)S(1)} %copy-done.2), custom_call_target="tpu_custom_call" | custom-call | tf_op jit(solution)/shard_map/rescale/pallas_call | solution.py:495
Async XLA Ops:
  0.0 48.9 %copy-start.2 = (f32[3,256]{1,0:T(4,128)S(1)}, f32[3,256]{1,0:T(4,128)}, u32[]{:S(2)}) copy-start(f32[3,256]{1,0:T(4,128)} %lower.1) | copy-start | bytes 9220
  0.0 48.9 %copy-start.1 = (f32[3,256]{1,0:T(4,128)S(1)}, f32[3,256]{1,0:T(4,128)}, u32[]{:S(2)}) copy-start(f32[3,256]{1,0:T(4,128)} %diagonal.1) | copy-start | bytes 9220
  0.0 49.0 %copy-start = (f32[3,256]{1,0:T(4,128)S(1)}, f32[3,256]{1,0:T(4,128)}, u32[]{:S(2)}) copy-start(f32[3,256]{1,0:T(4,128)} %profile.1) | copy-start | bytes 9220

commit v7 on v5

--- a/solution.py
+++ b/solution.py
@@ -13,7 +13,7 @@
 TSCALE = 8
 STEP = 2
 LAG = 5
-FIRST = 4
+FIRST = 5
 
 PAIRS = ((0, 0), (1, 0), (1, 1), (2, 0), (2, 1), (2, 2))
 SPREAD_FLOOR = 0.25

time: 51.7 us -> 51.8 us (level)
  no operation moved by 1% of the time
where the time goes in v7:
time: 51.8 us; the launch traced here: 51.7 us
  Pallas kernels  51.6 us (100%)
    pallas_call x1, Pallas kernels, shards(): pl.pallas_call(functools.partial(filter_kernel, n_wall, n_span), out_shap...  48.9 us
    pallas_call x1, Pallas kernels, shards(): pl.pallas_call(functools.partial(scale_kernel, float(n_samples * n_cols *...  2.7 us

profile of v7, /device:TPU:97, one launch (start us, length us, event | category | flops | bytes accessed | tf_op | source)
XLA Modules:
  0.0 51.7 jit_solution(11891480195022497632)
XLA Ops:
  0.0 0.0 copy-start.2
  0.0 0.0 copy-start.1
  0.0 0.0 copy-start
  0.0 48.9 %filters.1 = (f32[3,32,64,256]{3,2,1,0:T(8,128)S(1)}, f32[9,1,256]{2,1,0:T(1,128)S(1)}) custom-call(s32[3,32,64,256]{3,2,1,0:T(8,128)} %noise.1, s32[1,256]{1,0:T(1,128)} %bitcast.1), custom_call_target="tpu_custom_call" | custom-call | tf_op jit(solution)/shard_map/filters/pallas_call | solution.py:448
  49.0 0.0 copy-done.2
  49.0 0.0 copy-done.1
  49.0 0.0 copy-done
  49.0 2.7 %rescale.1 = f32[3,32,64,256]{3,2,1,0:T(8,128)} custom-call(f32[3,32,64,256]{3,2,1,0:T(8,128)S(1)} %get-tuple-element.7.fluct, f32[9,1,256]{2,1,0:T(1,128)S(1)} %get-tuple-element.8.totals, f32[3,256]{1,0:T(4,128)S(1)} %copy-done, f32[3,256]{1,0:T(4,128)S(1)} %copy-done.1, f32[3,256]{1,0:T(4,128)S(1)} %copy-done.2), custom_call_target="tpu_custom_call" | custom-call | tf_op jit(solution)/shard_map/rescale/pallas_call | solution.py:496
Async XLA Ops:
  0.0 49.0 %copy-start.2 = (f32[3,256]{1,0:T(4,128)S(1)}, f32[3,256]{1,0:T(4,128)}, u32[]{:S(2)}) copy-start(f32[3,256]{1,0:T(4,128)} %lower.1) | copy-start | bytes 9220
  0.0 49.0 %copy-start.1 = (f32[3,256]{1,0:T(4,128)S(1)}, f32[3,256]{1,0:T(4,128)}, u32[]{:S(2)}) copy-start(f32[3,256]{1,0:T(4,128)} %diagonal.1) | copy-start | bytes 9220
  0.0 49.0 %copy-start = (f32[3,256]{1,0:T(4,128)S(1)}, f32[3,256]{1,0:T(4,128)}, u32[]{:S(2)}) copy-start(f32[3,256]{1,0:T(4,128)} %profile.1) | copy-start | bytes 9220
